TPU v7x, 256 devices: a whole 4x4x8 slice. The times are simulated.
256 devices in a mesh: batch: 16 (over y, z_lo), mp: 16 (over z_hi, x, core).
Axes of the slice: x: 4, y: 4, z: 8 (z_hi: 2, z_lo: 4; z = z_hi * 4 + z_lo), core: 2. Of those that a mesh axis runs over, the one named last changes fastest.
Arguments:
- gate_act: bfloat16 [12288, 14336], P('batch', 'mp'), may hold values from -6 to 6
- up_act: bfloat16 [12288, 14336], P('batch', 'mp'), may hold values from -6 to 6
- upstream: bfloat16 [12288, 8192], P('batch', 'mp'), may hold values from -6 to 6
- kept_index: int32 [16, 16], P('batch'), may hold values from 0 to 31, as said below
- kept_count: int32 [16], P('batch'), may hold values from 1 to 16, as said below
Outputs:
- grad_down: bfloat16 [8192, 14336], P('batch', 'mp')
Inputs may be any that keep to these rules, and one draw needn't show every extreme that they name: `kept_index`: each group's row names different candidates; only the first kept_count entries of a row are kept. `kept_count`: the counts sum to 16 * 8 over the groups, and some group keeps exactly 16.
All inputs are finite; a program needn't handle non-finite values.
Results may differ from a plain program's by a relative error of at most 0.0049.
Values may be sent and summed in bfloat16 or wider, within the bound.
No kernel may reach another device: no remote copies, remote signals or barrier semaphores. Data moves between devices by JAX's collectives and lax.ppermute only.
A program may use at most 128 MiB of HBM per device.

v0:
```python
import math

import jax
import jax.numpy as jnp
from jax import lax
from jax.experimental import pallas as pl
from jax.experimental.pallas import tpu as pltpu
from jax.sharding import Mesh
from jax.sharding import PartitionSpec as P


SEQ = 24
CAND = 32
CAP = 8
F_CUTS = (512, 384)
E_CUTS = (256, 256)
SPREAD = ("zl", "zh", "x", "c")
SMEM = pl.BlockSpec(memory_space=pltpu.SMEM)
VMEM = pl.BlockSpec(memory_space=pltpu.VMEM)


def spread_pairs(sizes, flip):
    zl, zh, x, c = sizes

    def at(a, b, d, e):
        return ((a * zh + b) * x + d) * c + e

    pairs = []
    for z_from in range(zl):
        for h in range(zh):
            for i in range(x):
                for k in range(c):
                    z_to = (i % 2) * 2 + k
                    r = z_to ^ z_from
                    pairs.append((at(z_from, h, i, k), at(z_to, h ^ flip, (i // 2) * 2 + r // 2, r % 2)))
    return pairs


def swap(value, axis, bit):
    n = lax.axis_size(axis)
    return lax.ppermute(value, axis, [(i, i ^ bit) for i in range(n)])


def grads_body(rows, at_ref, own, rest, c_own, c_rest, out):
    width = own.shape[2]
    for s in range(4):
        for o in range(2):
            q = (s % 2) * 2 + o
            for k in range(2):
                d = (k * 2 + s // 2) ^ at_ref[0]
                source = (own, c_own)[o].at[k] if s == 0 else (rest, c_rest)[o].at[s - 1, k]
                columns = pl.ds(pl.multiple_of(d * width, 128), width)
                out[pl.ds(q * rows, rows), columns] = source[...]


def join_grads(first, own, rest, c_own, c_rest):
    rows, width = own.shape[1:]

    def body(*refs):
        grads_body(rows, *refs)

    return pl.pallas_call(
        body,
        out_shape=jax.ShapeDtypeStruct((4 * rows, 4 * width), own.dtype),
        in_specs=[SMEM, VMEM, VMEM, VMEM, VMEM],
        out_specs=VMEM,
        cost_estimate=pl.CostEstimate(flops=2_000_000_000, bytes_accessed=6_000_000, transcendentals=0),
    )(first, own, rest, c_own, c_rest)


def join_hidden(place, own, near, far, middle, passed):
    rows, width = own.shape

    def body(at_ref, own, near, far, middle, passed, out):
        def rows_of(r):
            return pl.ds(pl.multiple_of((r ^ at_ref[0]) * rows, rows), rows)

        out[rows_of(0), :] = own[...]
        out[rows_of(1), :] = near[...]
        out[rows_of(2), :] = far[...]

        @pl.when(at_ref[1] == 1)
        def _():
            out[rows_of(3), :] = middle[...]

        @pl.when(at_ref[1] == 0)
        def _():
            out[rows_of(3), :] = passed[...]

    return pl.pallas_call(
        body,
        out_shape=jax.ShapeDtypeStruct((4 * rows, width), own.dtype),
        in_specs=[SMEM, VMEM, VMEM, VMEM, VMEM, VMEM],
        out_specs=VMEM,
        cost_estimate=pl.CostEstimate(flops=1_000_000_000, bytes_accessed=3_000_000, transcendentals=0),
    )(place, own, near, far, middle, passed)


def on_device(gate_act, up_act, upstream, kept_index, kept_count):
    slots = kept_index.shape[1]
    rows = slots * SEQ
    hidden_width = gate_act.shape[1]
    model_part = upstream.shape[1]
    picked = kept_index[0]
    present = jnp.arange(slots, dtype=jnp.int32) < kept_count[0]
    y, z, zh, x, c = (lax.axis_index(a) for a in ("y", "zl", "zh", "x", "c"))
    sizes = tuple(lax.axis_size(a) for a in SPREAD)

    grads = upstream.reshape(CAND, SEQ, model_part)[picked].reshape(rows, model_part)
    owns, at = [], 0
    for width in E_CUTS:
        mine = grads[:, at : at + width]
        at += width
        got = []
        for k in (0, 1):
            got.append(lax.ppermute(mine, SPREAD, spread_pairs(sizes, k)))
        owns.append(jnp.stack(got))

    gate_all = gate_act.reshape(CAND, SEQ, hidden_width)
    up_all = up_act.reshape(CAND, SEQ, hidden_width)
    hidden = (
        jax.nn.silu(gate_all[picked].astype(jnp.float32)) * up_all[picked].astype(jnp.float32)
    ).astype(jnp.bfloat16)
    hidden = jnp.where(present[:, None, None], hidden, jnp.zeros_like(hidden)).reshape(rows, hidden_width)
    inner = ((z == 1) | (z == 2)).astype(jnp.int32)
    place = jnp.stack([(2 * (x % 2) + c).astype(jnp.int32), inner])
    hidden_parts, at = [], 0
    for width in F_CUTS:
        part = hidden[:, at : at + width]
        at += width
        far = swap(part, "zl", 2)
        near = swap(part, "zl", 1)
        middle = lax.ppermute(part, "zl", [(1, 2), (2, 1)])
        passed = lax.ppermute(far, "zl", [(2, 3), (1, 0)])
        hidden_parts.append(join_hidden(place, part, near, far, middle, passed))

    first = (((y // 2) ^ zh) * 2 + ((y % 2) ^ (x // 2))).astype(jnp.int32).reshape(1)
    grad_parts = []
    for own in owns:
        c_own = swap(own, "c", 1)
        rest = jnp.stack([swap(own, "x", s) for s in (1, 2, 3)])
        c_rest = swap(rest, "c", 1)
        grad_parts.append(join_grads(first, own, rest, c_own, c_rest))

    factor = 1.0 / math.sqrt(lax.axis_size("y") * lax.axis_size("zl") * CAP * SEQ)
    columns = []
    for h in hidden_parts:
        pieces = []
        for g in grad_parts:
            partial = lax.dot_general(
                g, h, (((0,), (0,)), ((), ())), preferred_element_type=jnp.float32
            ).astype(jnp.bfloat16)
            partial = partial.reshape(4, -1, h.shape[1])
            total = partial[0].astype(jnp.float32)
            for d in (1, 3, 2):
                total = total + swap(partial[d], "y", d).astype(jnp.float32)
            pieces.append((total * factor).astype(jnp.bfloat16))
        columns.append(jnp.concatenate(pieces, axis=0))
    return jnp.concatenate(columns, axis=1)


def solution(mesh):
    split = Mesh(mesh.devices.reshape(4, 4, 2, 4, 2), ("y", "zl", "zh", "x", "c"))
    batch, mp = ("y", "zl"), ("zh", "x", "c")
    in_specs = (P(batch, mp), P(batch, mp), P(batch, mp), P(batch, None), P(batch))

    return jax.shard_map(on_device, mesh=split, in_specs=in_specs, out_specs=P(batch, mp), check_vma=False)
```

profile of v0, /device:TPU:1, one launch (start us, length us, event | category | flops | bytes accessed | tf_op | source)
XLA Modules:
  0.0 200.8 jit_solution(15467119011425187799)
XLA Ops:
  3.2 7.3 %collective-permute-start.1 = (bf16[384,256]{1,0:T(8,128)(2,1)S(1)}, bf16[384,256]{1,0:T(8,128)(2,1)S(1)}, u32[]{:S(2)}, u32[]{:S(2)}) collective-permute-start(bf16[384,256]{1,0:T(8,128)(2,1)S(1)} %get-tuple-element.17), channel_id=1, source_target_pairs={{0,8},{1,25},{2,42},{3,59},{4,12},{5,29},{6,46},{7,63},{8,0},{9,17... | collective-permute-start | bytes 589832 | tf_op jit(solution)/shard_map/ppermute | solution.py:116
  10.5 3.6 %collective-permute-start = (bf16[384,256]{1,0:T(8,128)(2,1)S(1)}, bf16[384,256]{1,0:T(8,128)(2,1)S(1)}, u32[]{:S(2)}, u32[]{:S(2)}) collective-permute-start(bf16[384,256]{1,0:T(8,128)(2,1)S(1)} %get-tuple-element.17), channel_id=1, source_target_pairs={{0,0},{1,17},{2,34},{3,51},{4,4},{5,21},{6,38},{7,55},{8,8},{9,25}... | collective-permute-start | bytes 589832 | tf_op jit(solution)/shard_map/ppermute | solution.py:116
  14.1 2.5 %collective-permute-done.1 = bf16[384,256]{1,0:T(8,128)(2,1)S(1)} collective-permute-done((bf16[384,256]{1,0:T(8,128)(2,1)S(1)}, bf16[384,256]{1,0:T(8,128)(2,1)S(1)}, u32[]{:S(2)}, u32[]{:S(2)}) %collective-permute-start.1) | collective-permute-done | bytes 196640 | tf_op jit(solution)/shard_map/ppermute | solution.py:116
  18.5 8.9 %collective-permute-start.4 = (bf16[2,384,256]{2,1,0:T(8,128)(2,1)}, bf16[2,384,256]{2,1,0:T(8,128)(2,1)S(1)}, u32[]{:S(2)}, u32[]{:S(2)}) collective-permute-start(bf16[2,384,256]{2,1,0:T(8,128)(2,1)} %pad_maximum_fusion.2.refs_1_), channel_id=1, source_target_pairs={{0,6},{2,4},{4,2},{6,0},{1,7},{3,5},{5,3},{7,1},{8,14},{10,12},{12... | collective-permute-start | bytes 1179656 | tf_op jit(solution)/shard_map/ppermute | solution.py:41
  28.0 4.8 %collective-permute-start.15 = (bf16[384,256]{1,0:T(8,128)(2,1)}, bf16[384,256]{1,0:T(8,128)(2,1)}, u32[]{:S(2)}, u32[]{:S(2)}) collective-permute-start(bf16[384,256]{1,0:T(8,128)(2,1)} %get-tuple-element.18), channel_id=1, source_target_pairs={{0,8},{1,25},{2,42},{3,59},{4,12},{5,29},{6,46},{7,63},{8,0},{9,17... | collective-permute-start | bytes 589832 | tf_op jit(solution)/shard_map/ppermute | solution.py:116
  32.8 4.1 %collective-permute-start.14 = (bf16[384,256]{1,0:T(8,128)(2,1)}, bf16[384,256]{1,0:T(8,128)(2,1)}, u32[]{:S(2)}, u32[]{:S(2)}) collective-permute-start(bf16[384,256]{1,0:T(8,128)(2,1)} %get-tuple-element.18), channel_id=1, source_target_pairs={{0,0},{1,17},{2,34},{3,51},{4,4},{5,21},{6,38},{7,55},{8,8},{9,25}... | collective-permute-start | bytes 589832 | tf_op jit(solution)/shard_map/ppermute | solution.py:116
  40.5 4.2 %collective-permute-done.4 = bf16[2,384,256]{2,1,0:T(8,128)(2,1)S(1)} collective-permute-done((bf16[2,384,256]{2,1,0:T(8,128)(2,1)}, bf16[2,384,256]{2,1,0:T(8,128)(2,1)S(1)}, u32[]{:S(2)}, u32[]{:S(2)}) %collective-permute-start.4) | collective-permute-done | bytes 393248 | tf_op jit(solution)/shard_map/ppermute | solution.py:41
  44.7 6.4 %collective-permute-done.2 = bf16[2,384,256]{2,1,0:T(8,128)(2,1)} collective-permute-done((bf16[2,384,256]{2,1,0:T(8,128)(2,1)}, bf16[2,384,256]{2,1,0:T(8,128)(2,1)}, u32[]{:S(2)}, u32[]{:S(2)}) %collective-permute-start.2) | collective-permute-done | bytes 393248 | tf_op jit(solution)/shard_map/ppermute | solution.py:41
  53.3 3.0 %collective-permute-start.6 = (bf16[3,2,384,256]{3,2,1,0:T(8,128)(2,1)}, bf16[3,2,384,256]{3,2,1,0:T(8,128)(2,1)}, u32[]{:S(2)}, u32[]{:S(2)}) collective-permute-start(bf16[3,2,384,256]{3,2,1,0:T(8,128)(2,1)} %pad_maximum_fusion.refs_2_), channel_id=1, source_target_pairs={{0,1},{1,0},{2,3},{3,2},{4,5},{5,4},{6,7},{7,6},{8,9},{9,8},{10,11... | collective-permute-start | bytes 3538952 | tf_op jit(solution)/shard_map/ppermute | solution.py:41
  57.6 3.2 %collective-permute-start.25 = (bf16[384,384]{1,0:T(8,128)(2,1)S(1)}, bf16[384,384]{1,0:T(8,128)(2,1)S(1)}, u32[]{:S(2)}, u32[]{:S(2)}) collective-permute-start(bf16[384,384]{1,0:T(8,128)(2,1)S(1)} %slice.113.own), channel_id=1, source_target_pairs={{0,32},{16,48},{32,0},{48,16},{1,33},{17,49},{33,1},{49,17},{2,34}... | collective-permute-start | bytes 884744 | tf_op jit(solution)/shard_map/ppermute | solution.py:41
  64.8 3.2 %collective-permute-start.18 = (bf16[2,384,256]{2,1,0:T(8,128)(2,1)}, bf16[2,384,256]{2,1,0:T(8,128)(2,1)S(1)}, u32[]{:S(2)}, u32[]{:S(2)}) collective-permute-start(bf16[2,384,256]{2,1,0:T(8,128)(2,1)} %pad_maximum_fusion.3.refs_1_), channel_id=1, source_target_pairs={{0,6},{2,4},{4,2},{6,0},{1,7},{3,5},{5,3},{7,1},{8,14},{10,12},{12... | collective-permute-start | bytes 1179656 | tf_op jit(solution)/shard_map/ppermute | solution.py:41
  67.9 20.9 %collective-permute-done.25.far = bf16[384,384]{1,0:T(8,128)(2,1)S(1)} collective-permute-done((bf16[384,384]{1,0:T(8,128)(2,1)S(1)}, bf16[384,384]{1,0:T(8,128)(2,1)S(1)}, u32[]{:S(2)}, u32[]{:S(2)}) %collective-permute-start.25) | collective-permute-done | bytes 294944 | tf_op jit(solution)/shard_map/ppermute | solution.py:41
  88.8 2.4 %collective-permute-start.17 = (bf16[2,384,256]{2,1,0:T(8,128)(2,1)}, bf16[2,384,256]{2,1,0:T(8,128)(2,1)S(1)}, u32[]{:S(2)}, u32[]{:S(2)}) collective-permute-start(bf16[2,384,256]{2,1,0:T(8,128)(2,1)} %pad_maximum_fusion.3.refs_1_), channel_id=1, source_target_pairs={{0,4},{2,6},{4,0},{6,2},{1,5},{3,7},{5,1},{7,3},{8,12},{10,14},{12... | collective-permute-start | bytes 1179656 | tf_op jit(solution)/shard_map/ppermute | solution.py:41
  92.8 4.5 %collective-permute-done.8.far = bf16[384,512]{1,0:T(8,128)(2,1)} collective-permute-done((bf16[384,512]{1,0:T(8,128)(2,1)}, bf16[384,512]{1,0:T(8,128)(2,1)}, u32[]{:S(2)}, u32[]{:S(2)}) %collective-permute-start.8) | collective-permute-done | bytes 393248 | tf_op jit(solution)/shard_map/ppermute | solution.py:41
  100.1 3.4 %collective-permute-start.7 = (bf16[384,512]{1,0:T(8,128)(2,1)}, bf16[384,512]{1,0:T(8,128)(2,1)}, u32[]{:S(2)}, u32[]{:S(2)}) collective-permute-start(bf16[384,512]{1,0:T(8,128)(2,1)} %slice.103.own), channel_id=1, source_target_pairs={{0,16},{16,0},{32,48},{48,32},{1,17},{17,1},{33,49},{49,33},{2,18}... | collective-permute-start | bytes 1179656 | tf_op jit(solution)/shard_map/ppermute | solution.py:41
  103.4 6.0 %collective-permute-done.16 = bf16[2,384,256]{2,1,0:T(8,128)(2,1)S(1)} collective-permute-done((bf16[2,384,256]{2,1,0:T(8,128)(2,1)}, bf16[2,384,256]{2,1,0:T(8,128)(2,1)S(1)}, u32[]{:S(2)}, u32[]{:S(2)}) %collective-permute-start.16) | collective-permute-done | bytes 393248 | tf_op jit(solution)/shard_map/ppermute | solution.py:41
  113.6 2.6 %shard_map.58 = bf16[1536,384]{1,0:T(8,128)(2,1)} custom-call(s32[2]{0:T(128)} %pad_add_fusion.at_ref, bf16[384,384]{1,0:T(8,128)(2,1)} %copy-done.4, bf16[384,384]{1,0:T(8,128)(2,1)} %collective-permute-done.24.near, bf16[384,384]{1,0:T(8,128)(2,1)} %copy-done.6, bf16[384,384]{1,0:T(8,128)(2,1)} %copy-done.5, bf16[384,384]{1,0:T(8,128)(2,1)} %collective-permute-done.27.passed), custom_call_target="tpu_custom_call" | custom-call | flops 1000000000 | bytes 3000000 | tf_op jit(solution)/shard_map/pallas_call | solution.py:90
  118.5 5.4 %collective-permute-done.10.passed = bf16[384,512]{1,0:T(8,128)(2,1)} collective-permute-done((bf16[384,512]{1,0:T(8,128)(2,1)}, bf16[384,512]{1,0:T(8,128)(2,1)}, u32[]{:S(2)}, u32[]{:S(2)}) %collective-permute-start.10) | collective-permute-done | bytes 393248 | tf_op jit(solution)/shard_map/ppermute | solution.py:134
  123.9 2.9 %shard_map.56 = bf16[1536,512]{1,0:T(8,128)(2,1)} custom-call(s32[2]{0:T(128)} %pad_add_fusion.at_ref, bf16[384,512]{1,0:T(8,128)(2,1)} %slice.103.own, bf16[384,512]{1,0:T(8,128)(2,1)} %collective-permute-done.7.near, bf16[384,512]{1,0:T(8,128)(2,1)} %collective-permute-done.8.far, bf16[384,512]{1,0:T(8,128)(2,1)} %collective-permute-done.9.middle, ...), custom_call_target="tpu_custom_call" | custom-call | flops 1000000000 | bytes 3000000 | tf_op jit(solution)/shard_map/pallas_call | solution.py:90
  126.8 3.9 %shard_map.55 = bf16[1536,1024]{1,0:T(8,128)(2,1)} custom-call(s32[1]{0:T(128)} %bitcast.refs_0_, bf16[2,384,256]{2,1,0:T(8,128)(2,1)} %pad_maximum_fusion.2.refs_1_, bf16[3,2,384,256]{3,2,1,0:T(8,128)(2,1)} %pad_maximum_fusion.refs_2_, bf16[2,384,256]{2,1,0:T(8,128)(2,1)} %collective-permute-done.5.refs_3_, ...), custom_call_target="tpu_custom_call" | custom-call | flops 2000000000 | bytes 6000000 | tf_op jit(solution)/shard_map/pallas_call | solution.py:62
  130.7 5.3 %convolution_convert_fusion.1 = bf16[1024,512]{1,0:T(8,128)(2,1)} fusion(bf16[1536,1024]{1,0:T(8,128)(2,1)} %shard_map.55, bf16[1536,512]{1,0:T(8,128)(2,1)} %shard_map.56), kind=kOutput, calls=%fused_computation.6 | convolution fusion | flops 1611137024 | bytes 5767168 | tf_op jit(solution)/shard_map/dot_general | solution.py:150
  137.9 3.9 %shard_map.57 = bf16[1536,1024]{1,0:T(8,128)(2,1)} custom-call(s32[1]{0:T(128)} %bitcast.refs_0_, bf16[2,384,256]{2,1,0:T(8,128)(2,1)} %pad_maximum_fusion.3.refs_1_, bf16[3,2,384,256]{3,2,1,0:T(8,128)(2,1)} %copy-done.1, bf16[2,384,256]{2,1,0:T(8,128)(2,1)} %collective-permute-done.19.refs_3_, bf16[3,2,384,256]{3,2,1,0:T(8,128)(2,1)} %collective-permute-done.20.refs_4_), custom_call_target="tpu_custom_call" | custom-call | flops 2000000000 | bytes 6000000 | tf_op jit(solution)/shard_map/pallas_call | solution.py:62
  141.8 4.3 %convolution_convert_fusion = bf16[1024,512]{1,0:T(8,128)(2,1)S(1)} fusion(bf16[1536,1024]{1,0:T(8,128)(2,1)} %shard_map.57, bf16[1536,512]{1,0:T(8,128)(2,1)} %shard_map.56), kind=kOutput, calls=%fused_computation.5 | convolution fusion | flops 1611137024 | bytes 5767168 | tf_op jit(solution)/shard_map/dot_general | solution.py:150
  149.5 2.6 %collective-permute-start.30 = (bf16[256,384]{1,0:T(8,128)(2,1)S(1)}, bf16[256,384]{1,0:T(8,128)(2,1)S(1)}, u32[]{:S(2)}, u32[]{:S(2)}) collective-permute-start(bf16[256,384]{1,0:T(8,128)(2,1)S(1)} %get-tuple-element.12), channel_id=1, source_target_pairs={{0,128},{64,192},{128,0},{192,64},{1,129},{65,193},{129,1},{193,65... | collective-permute-start | bytes 589832 | tf_op jit(solution)/shard_map/ppermute | solution.py:41
  153.9 2.5 %collective-permute-start.13 = (bf16[256,512]{1,0:T(8,128)(2,1)S(1)}, bf16[256,512]{1,0:T(8,128)(2,1)S(1)}, u32[]{:S(2)}, u32[]{:S(2)}) collective-permute-start(bf16[256,512]{1,0:T(8,128)(2,1)S(1)} %get-tuple-element.6), channel_id=1, source_target_pairs={{0,128},{64,192},{128,0},{192,64},{1,129},{65,193},{129,1},{193,65... | collective-permute-start | bytes 786440 | tf_op jit(solution)/shard_map/ppermute | solution.py:41
  156.4 2.9 %collective-permute-done.30 = bf16[256,384]{1,0:T(8,128)(2,1)S(1)} collective-permute-done((bf16[256,384]{1,0:T(8,128)(2,1)S(1)}, bf16[256,384]{1,0:T(8,128)(2,1)S(1)}, u32[]{:S(2)}, u32[]{:S(2)}) %collective-permute-start.30) | collective-permute-done | bytes 196640 | tf_op jit(solution)/shard_map/ppermute | solution.py:41
  161.6 5.7 %collective-permute-done.31 = bf16[256,384]{1,0:T(8,128)(2,1)S(1)} collective-permute-done((bf16[256,384]{1,0:T(8,128)(2,1)S(1)}, bf16[256,384]{1,0:T(8,128)(2,1)S(1)}, u32[]{:S(2)}, u32[]{:S(2)}) %collective-permute-start.31) | collective-permute-done | bytes 196640 | tf_op jit(solution)/shard_map/ppermute | solution.py:41
  167.2 2.5 %collective-permute-start.32 = (bf16[256,384]{1,0:T(8,128)(2,1)S(1)}, bf16[256,384]{1,0:T(8,128)(2,1)S(1)}, u32[]{:S(2)}, u32[]{:S(2)}) collective-permute-start(bf16[256,384]{1,0:T(8,128)(2,1)S(1)} %get-tuple-element.16), channel_id=1, source_target_pairs={{0,192},{64,128},{128,64},{192,0},{1,193},{65,129},{129,65},{193,1... | collective-permute-start | bytes 589832 | tf_op jit(solution)/shard_map/ppermute | solution.py:41
  169.8 9.5 %collective-permute-done.33 = bf16[256,384]{1,0:T(8,128)(2,1)S(1)} collective-permute-done((bf16[256,384]{1,0:T(8,128)(2,1)S(1)}, bf16[256,384]{1,0:T(8,128)(2,1)S(1)}, u32[]{:S(2)}, u32[]{:S(2)}) %collective-permute-start.33) | collective-permute-done | bytes 196640 | tf_op jit(solution)/shard_map/ppermute | solution.py:41
  179.3 5.0 %collective-permute-done.32 = bf16[256,384]{1,0:T(8,128)(2,1)S(1)} collective-permute-done((bf16[256,384]{1,0:T(8,128)(2,1)S(1)}, bf16[256,384]{1,0:T(8,128)(2,1)S(1)}, u32[]{:S(2)}, u32[]{:S(2)}) %collective-permute-start.32) | collective-permute-done | bytes 196640 | tf_op jit(solution)/shard_map/ppermute | solution.py:41
  186.0 6.1 %collective-permute-done.23 = bf16[256,512]{1,0:T(8,128)(2,1)S(1)} collective-permute-done((bf16[256,512]{1,0:T(8,128)(2,1)S(1)}, bf16[256,512]{1,0:T(8,128)(2,1)S(1)}, u32[]{:S(2)}, u32[]{:S(2)}) %collective-permute-start.23) | collective-permute-done | bytes 262176 | tf_op jit(solution)/shard_map/ppermute | solution.py:41
  192.2 7.5 %collective-permute-done.22 = bf16[256,512]{1,0:T(8,128)(2,1)S(1)} collective-permute-done((bf16[256,512]{1,0:T(8,128)(2,1)S(1)}, bf16[256,512]{1,0:T(8,128)(2,1)S(1)}, u32[]{:S(2)}, u32[]{:S(2)}) %collective-permute-start.22) | collective-permute-done | bytes 262176 | tf_op jit(solution)/shard_map/ppermute | solution.py:41
  (92 shorter events, 38.7 us)
Async XLA Ops:
  3.2 13.5 %collective-permute-start.1 = (bf16[384,256]{1,0:T(8,128)(2,1)S(1)}, bf16[384,256]{1,0:T(8,128)(2,1)S(1)}, u32[]{:S(2)}, u32[]{:S(2)}) collective-permute-start(bf16[384,256]{1,0:T(8,128)(2,1)S(1)} %get-tuple-element.17), channel_id=1, source_target_pairs={{0,8},{1,25},{2,42},{3,59},{4,12},{5,29},{6,46},{7,63},{8,0},{9,17... | collective-permute-start | bytes 589832 | tf_op jit(solution)/shard_map/ppermute | solution.py:116
  10.5 7.3 %collective-permute-start = (bf16[384,256]{1,0:T(8,128)(2,1)S(1)}, bf16[384,256]{1,0:T(8,128)(2,1)S(1)}, u32[]{:S(2)}, u32[]{:S(2)}) collective-permute-start(bf16[384,256]{1,0:T(8,128)(2,1)S(1)} %get-tuple-element.17), channel_id=1, source_target_pairs={{0,0},{1,17},{2,34},{3,51},{4,4},{5,21},{6,38},{7,55},{8,8},{9,25}... | collective-permute-start | bytes 589832 | tf_op jit(solution)/shard_map/ppermute | solution.py:116
  18.5 26.1 %collective-permute-start.4 = (bf16[2,384,256]{2,1,0:T(8,128)(2,1)}, bf16[2,384,256]{2,1,0:T(8,128)(2,1)S(1)}, u32[]{:S(2)}, u32[]{:S(2)}) collective-permute-start(bf16[2,384,256]{2,1,0:T(8,128)(2,1)} %pad_maximum_fusion.2.refs_1_), channel_id=1, source_target_pairs={{0,6},{2,4},{4,2},{6,0},{1,7},{3,5},{5,3},{7,1},{8,14},{10,12},{12... | collective-permute-start | bytes 1179656 | tf_op jit(solution)/shard_map/ppermute | solution.py:41
  27.4 17.3 %collective-permute-start.3 = (bf16[2,384,256]{2,1,0:T(8,128)(2,1)}, bf16[2,384,256]{2,1,0:T(8,128)(2,1)S(1)}, u32[]{:S(2)}, u32[]{:S(2)}) collective-permute-start(bf16[2,384,256]{2,1,0:T(8,128)(2,1)} %pad_maximum_fusion.2.refs_1_), channel_id=1, source_target_pairs={{0,4},{2,6},{4,0},{6,2},{1,5},{3,7},{5,1},{7,3},{8,12},{10,14},{12... | collective-permute-start | bytes 1179656 | tf_op jit(solution)/shard_map/ppermute | solution.py:41
  27.6 23.5 %collective-permute-start.2 = (bf16[2,384,256]{2,1,0:T(8,128)(2,1)}, bf16[2,384,256]{2,1,0:T(8,128)(2,1)}, u32[]{:S(2)}, u32[]{:S(2)}) collective-permute-start(bf16[2,384,256]{2,1,0:T(8,128)(2,1)} %pad_maximum_fusion.2.refs_1_), channel_id=1, source_target_pairs={{0,2},{2,0},{4,6},{6,4},{1,3},{3,1},{5,7},{7,5},{8,10},{10,8},{12,... | collective-permute-start | bytes 1179656 | tf_op jit(solution)/shard_map/ppermute | solution.py:41
  28.0 32.8 %collective-permute-start.15 = (bf16[384,256]{1,0:T(8,128)(2,1)}, bf16[384,256]{1,0:T(8,128)(2,1)}, u32[]{:S(2)}, u32[]{:S(2)}) collective-permute-start(bf16[384,256]{1,0:T(8,128)(2,1)} %get-tuple-element.18), channel_id=1, source_target_pairs={{0,8},{1,25},{2,42},{3,59},{4,12},{5,29},{6,46},{7,63},{8,0},{9,17... | collective-permute-start | bytes 589832 | tf_op jit(solution)/shard_map/ppermute | solution.py:116
  32.8 28.9 %collective-permute-start.14 = (bf16[384,256]{1,0:T(8,128)(2,1)}, bf16[384,256]{1,0:T(8,128)(2,1)}, u32[]{:S(2)}, u32[]{:S(2)}) collective-permute-start(bf16[384,256]{1,0:T(8,128)(2,1)} %get-tuple-element.18), channel_id=1, source_target_pairs={{0,0},{1,17},{2,34},{3,51},{4,4},{5,21},{6,38},{7,55},{8,8},{9,25}... | collective-permute-start | bytes 589832 | tf_op jit(solution)/shard_map/ppermute | solution.py:116
  53.3 73.5 %collective-permute-start.6 = (bf16[3,2,384,256]{3,2,1,0:T(8,128)(2,1)}, bf16[3,2,384,256]{3,2,1,0:T(8,128)(2,1)}, u32[]{:S(2)}, u32[]{:S(2)}) collective-permute-start(bf16[3,2,384,256]{3,2,1,0:T(8,128)(2,1)} %pad_maximum_fusion.refs_2_), channel_id=1, source_target_pairs={{0,1},{1,0},{2,3},{3,2},{4,5},{5,4},{6,7},{7,6},{8,9},{9,8},{10,11... | collective-permute-start | bytes 3538952 | tf_op jit(solution)/shard_map/ppermute | solution.py:41
  56.9 7.9 %collective-permute-start.26 = (bf16[384,384]{1,0:T(8,128)(2,1)S(1)}, bf16[384,384]{1,0:T(8,128)(2,1)S(1)}, u32[]{:S(2)}, u32[]{:S(2)}) collective-permute-start(bf16[384,384]{1,0:T(8,128)(2,1)S(1)} %slice.113.own), channel_id=1, source_target_pairs={{16,32},{32,16},{17,33},{33,17},{18,34},{34,18},{19,35},{35,19},{2... | collective-permute-start | bytes 884744 | tf_op jit(solution)/shard_map/ppermute | solution.py:133
  57.6 31.2 %collective-permute-start.25 = (bf16[384,384]{1,0:T(8,128)(2,1)S(1)}, bf16[384,384]{1,0:T(8,128)(2,1)S(1)}, u32[]{:S(2)}, u32[]{:S(2)}) collective-permute-start(bf16[384,384]{1,0:T(8,128)(2,1)S(1)} %slice.113.own), channel_id=1, source_target_pairs={{0,32},{16,48},{32,0},{48,16},{1,33},{17,49},{33,1},{49,17},{2,34}... | collective-permute-start | bytes 884744 | tf_op jit(solution)/shard_map/ppermute | solution.py:41
  60.7 30.5 %collective-permute-start.24 = (bf16[384,384]{1,0:T(8,128)(2,1)S(1)}, bf16[384,384]{1,0:T(8,128)(2,1)}, u32[]{:S(2)}, u32[]{:S(2)}) collective-permute-start(bf16[384,384]{1,0:T(8,128)(2,1)S(1)} %slice.113.own), channel_id=1, source_target_pairs={{0,16},{16,0},{32,48},{48,32},{1,17},{17,1},{33,49},{49,33},{2,18}... | collective-permute-start | bytes 884744 | tf_op jit(solution)/shard_map/ppermute | solution.py:41
  61.7 35.7 %collective-permute-start.8 = (bf16[384,512]{1,0:T(8,128)(2,1)}, bf16[384,512]{1,0:T(8,128)(2,1)}, u32[]{:S(2)}, u32[]{:S(2)}) collective-permute-start(bf16[384,512]{1,0:T(8,128)(2,1)} %slice.103.own), channel_id=1, source_target_pairs={{0,32},{16,48},{32,0},{48,16},{1,33},{17,49},{33,1},{49,17},{2,34}... | collective-permute-start | bytes 1179656 | tf_op jit(solution)/shard_map/ppermute | solution.py:41
  64.8 33.8 %collective-permute-start.18 = (bf16[2,384,256]{2,1,0:T(8,128)(2,1)}, bf16[2,384,256]{2,1,0:T(8,128)(2,1)S(1)}, u32[]{:S(2)}, u32[]{:S(2)}) collective-permute-start(bf16[2,384,256]{2,1,0:T(8,128)(2,1)} %pad_maximum_fusion.3.refs_1_), channel_id=1, source_target_pairs={{0,6},{2,4},{4,2},{6,0},{1,7},{3,5},{5,3},{7,1},{8,14},{10,12},{12... | collective-permute-start | bytes 1179656 | tf_op jit(solution)/shard_map/ppermute | solution.py:41
  88.8 11.3 %collective-permute-start.17 = (bf16[2,384,256]{2,1,0:T(8,128)(2,1)}, bf16[2,384,256]{2,1,0:T(8,128)(2,1)S(1)}, u32[]{:S(2)}, u32[]{:S(2)}) collective-permute-start(bf16[2,384,256]{2,1,0:T(8,128)(2,1)} %pad_maximum_fusion.3.refs_1_), channel_id=1, source_target_pairs={{0,4},{2,6},{4,0},{6,2},{1,5},{3,7},{5,1},{7,3},{8,12},{10,14},{12... | collective-permute-start | bytes 1179656 | tf_op jit(solution)/shard_map/ppermute | solution.py:41
  91.2 18.2 %collective-permute-start.16 = (bf16[2,384,256]{2,1,0:T(8,128)(2,1)}, bf16[2,384,256]{2,1,0:T(8,128)(2,1)S(1)}, u32[]{:S(2)}, u32[]{:S(2)}) collective-permute-start(bf16[2,384,256]{2,1,0:T(8,128)(2,1)} %pad_maximum_fusion.3.refs_1_), channel_id=1, source_target_pairs={{0,2},{2,0},{4,6},{6,4},{1,3},{3,1},{5,7},{7,5},{8,10},{10,8},{12,... | collective-permute-start | bytes 1179656 | tf_op jit(solution)/shard_map/ppermute | solution.py:41
  97.3 13.4 %collective-permute-start.27 = (bf16[384,384]{1,0:T(8,128)(2,1)S(1)}, bf16[384,384]{1,0:T(8,128)(2,1)}, u32[]{:S(2)}, u32[]{:S(2)}) collective-permute-start(bf16[384,384]{1,0:T(8,128)(2,1)S(1)} %collective-permute-done.25.far), channel_id=1, source_target_pairs={{32,48},{16,0},{33,49},{17,1},{34,50},{18,2},{35,51},{19,3},{36,52... | collective-permute-start | bytes 884744 | tf_op jit(solution)/shard_map/ppermute | solution.py:134
  98.6 18.7 %collective-permute-start.9 = (bf16[384,512]{1,0:T(8,128)(2,1)}, bf16[384,512]{1,0:T(8,128)(2,1)}, u32[]{:S(2)}, u32[]{:S(2)}) collective-permute-start(bf16[384,512]{1,0:T(8,128)(2,1)} %slice.103.own), channel_id=1, source_target_pairs={{16,32},{32,16},{17,33},{33,17},{18,34},{34,18},{19,35},{35,19},{2... | collective-permute-start | bytes 1179656 | tf_op jit(solution)/shard_map/ppermute | solution.py:133
  100.1 17.4 %collective-permute-start.7 = (bf16[384,512]{1,0:T(8,128)(2,1)}, bf16[384,512]{1,0:T(8,128)(2,1)}, u32[]{:S(2)}, u32[]{:S(2)}) collective-permute-start(bf16[384,512]{1,0:T(8,128)(2,1)} %slice.103.own), channel_id=1, source_target_pairs={{0,16},{16,0},{32,48},{48,32},{1,17},{17,1},{33,49},{49,33},{2,18}... | collective-permute-start | bytes 1179656 | tf_op jit(solution)/shard_map/ppermute | solution.py:41
  109.4 14.4 %collective-permute-start.10 = (bf16[384,512]{1,0:T(8,128)(2,1)}, bf16[384,512]{1,0:T(8,128)(2,1)}, u32[]{:S(2)}, u32[]{:S(2)}) collective-permute-start(bf16[384,512]{1,0:T(8,128)(2,1)} %collective-permute-done.8.far), channel_id=1, source_target_pairs={{32,48},{16,0},{33,49},{17,1},{34,50},{18,2},{35,51},{19,3},{36,52... | collective-permute-start | bytes 1179656 | tf_op jit(solution)/shard_map/ppermute | solution.py:134
  110.8 16.0 %collective-permute-start.5 = (bf16[2,384,256]{2,1,0:T(8,128)(2,1)}, bf16[2,384,256]{2,1,0:T(8,128)(2,1)}, u32[]{:S(2)}, u32[]{:S(2)}) collective-permute-start(bf16[2,384,256]{2,1,0:T(8,128)(2,1)} %pad_maximum_fusion.2.refs_1_), channel_id=1, source_target_pairs={{0,1},{1,0},{2,3},{3,2},{4,5},{5,4},{6,7},{7,6},{8,9},{9,8},{10,11... | collective-permute-start | bytes 1179656 | tf_op jit(solution)/shard_map/ppermute | solution.py:41
  117.3 20.6 %collective-permute-start.19 = (bf16[2,384,256]{2,1,0:T(8,128)(2,1)}, bf16[2,384,256]{2,1,0:T(8,128)(2,1)}, u32[]{:S(2)}, u32[]{:S(2)}) collective-permute-start(bf16[2,384,256]{2,1,0:T(8,128)(2,1)} %pad_maximum_fusion.3.refs_1_), channel_id=1, source_target_pairs={{0,1},{1,0},{2,3},{3,2},{4,5},{5,4},{6,7},{7,6},{8,9},{9,8},{10,11... | collective-permute-start | bytes 1179656 | tf_op jit(solution)/shard_map/ppermute | solution.py:41
  117.5 20.5 %collective-permute-start.20 = (bf16[3,2,384,256]{3,2,1,0:T(8,128)(2,1)S(1)}, bf16[3,2,384,256]{3,2,1,0:T(8,128)(2,1)}, u32[]{:S(2)}, u32[]{:S(2)}) collective-permute-start(bf16[3,2,384,256]{3,2,1,0:T(8,128)(2,1)S(1)} %pad_maximum_fusion.1.refs_2_), channel_id=1, source_target_pairs={{0,1},{1,0},{2,3},{3,2},{4,5},{5,4},{6,7},{7,6},{8,9},{9,8},{10,11... | collective-permute-start | bytes 3538952 | tf_op jit(solution)/shard_map/ppermute | solution.py:41
  149.5 9.8 %collective-permute-start.30 = (bf16[256,384]{1,0:T(8,128)(2,1)S(1)}, bf16[256,384]{1,0:T(8,128)(2,1)S(1)}, u32[]{:S(2)}, u32[]{:S(2)}) collective-permute-start(bf16[256,384]{1,0:T(8,128)(2,1)S(1)} %get-tuple-element.12), channel_id=1, source_target_pairs={{0,128},{64,192},{128,0},{192,64},{1,129},{65,193},{129,1},{193,65... | collective-permute-start | bytes 589832 | tf_op jit(solution)/shard_map/ppermute | solution.py:41
  152.1 9.5 %collective-permute-start.29 = (bf16[256,384]{1,0:T(8,128)(2,1)S(1)}, bf16[256,384]{1,0:T(8,128)(2,1)S(1)}, u32[]{:S(2)}, u32[]{:S(2)}) collective-permute-start(bf16[256,384]{1,0:T(8,128)(2,1)S(1)} %get-tuple-element.13), channel_id=1, source_target_pairs={{0,192},{64,128},{128,64},{192,0},{1,193},{65,129},{129,65},{193,1... | collective-permute-start | bytes 589832 | tf_op jit(solution)/shard_map/ppermute | solution.py:41
  152.2 32.7 %collective-permute-start.11 = (bf16[256,512]{1,0:T(8,128)(2,1)S(1)}, bf16[256,512]{1,0:T(8,128)(2,1)S(1)}, u32[]{:S(2)}, u32[]{:S(2)}) collective-permute-start(bf16[256,512]{1,0:T(8,128)(2,1)S(1)} %get-tuple-element.5), channel_id=1, source_target_pairs={{0,64},{64,0},{128,192},{192,128},{1,65},{65,1},{129,193},{193,129... | collective-permute-start | bytes 786440 | tf_op jit(solution)/shard_map/ppermute | solution.py:41
  152.3 14.9 %collective-permute-start.31 = (bf16[256,384]{1,0:T(8,128)(2,1)S(1)}, bf16[256,384]{1,0:T(8,128)(2,1)S(1)}, u32[]{:S(2)}, u32[]{:S(2)}) collective-permute-start(bf16[256,384]{1,0:T(8,128)(2,1)S(1)} %get-tuple-element.14), channel_id=1, source_target_pairs={{0,64},{64,0},{128,192},{192,128},{1,65},{65,1},{129,193},{193,129... | collective-permute-start | bytes 589832 | tf_op jit(solution)/shard_map/ppermute | solution.py:41
  153.9 31.9 %collective-permute-start.13 = (bf16[256,512]{1,0:T(8,128)(2,1)S(1)}, bf16[256,512]{1,0:T(8,128)(2,1)S(1)}, u32[]{:S(2)}, u32[]{:S(2)}) collective-permute-start(bf16[256,512]{1,0:T(8,128)(2,1)S(1)} %get-tuple-element.6), channel_id=1, source_target_pairs={{0,128},{64,192},{128,0},{192,64},{1,129},{65,193},{129,1},{193,65... | collective-permute-start | bytes 786440 | tf_op jit(solution)/shard_map/ppermute | solution.py:41
  159.3 26.5 %collective-permute-start.12 = (bf16[256,512]{1,0:T(8,128)(2,1)S(1)}, bf16[256,512]{1,0:T(8,128)(2,1)S(1)}, u32[]{:S(2)}, u32[]{:S(2)}) collective-permute-start(bf16[256,512]{1,0:T(8,128)(2,1)S(1)} %get-tuple-element.7), channel_id=1, source_target_pairs={{0,192},{64,128},{128,64},{192,0},{1,193},{65,129},{129,65},{193,1... | collective-permute-start | bytes 786440 | tf_op jit(solution)/shard_map/ppermute | solution.py:41
  161.6 17.7 %collective-permute-start.33 = (bf16[256,384]{1,0:T(8,128)(2,1)S(1)}, bf16[256,384]{1,0:T(8,128)(2,1)S(1)}, u32[]{:S(2)}, u32[]{:S(2)}) collective-permute-start(bf16[256,384]{1,0:T(8,128)(2,1)S(1)} %get-tuple-element.15), channel_id=1, source_target_pairs={{0,128},{64,192},{128,0},{192,64},{1,129},{65,193},{129,1},{193,65... | collective-permute-start | bytes 589832 | tf_op jit(solution)/shard_map/ppermute | solution.py:41
  167.2 17.1 %collective-permute-start.32 = (bf16[256,384]{1,0:T(8,128)(2,1)S(1)}, bf16[256,384]{1,0:T(8,128)(2,1)S(1)}, u32[]{:S(2)}, u32[]{:S(2)}) collective-permute-start(bf16[256,384]{1,0:T(8,128)(2,1)S(1)} %get-tuple-element.16), channel_id=1, source_target_pairs={{0,192},{64,128},{128,64},{192,0},{1,193},{65,129},{129,65},{193,1... | collective-permute-start | bytes 589832 | tf_op jit(solution)/shard_map/ppermute | solution.py:41
  184.3 7.8 %collective-permute-start.23 = (bf16[256,512]{1,0:T(8,128)(2,1)S(1)}, bf16[256,512]{1,0:T(8,128)(2,1)S(1)}, u32[]{:S(2)}, u32[]{:S(2)}) collective-permute-start(bf16[256,512]{1,0:T(8,128)(2,1)S(1)} %get-tuple-element.9), channel_id=1, source_target_pairs={{0,128},{64,192},{128,0},{192,64},{1,129},{65,193},{129,1},{193,65... | collective-permute-start | bytes 786440 | tf_op jit(solution)/shard_map/ppermute | solution.py:41
  184.9 14.8 %collective-permute-start.22 = (bf16[256,512]{1,0:T(8,128)(2,1)S(1)}, bf16[256,512]{1,0:T(8,128)(2,1)S(1)}, u32[]{:S(2)}, u32[]{:S(2)}) collective-permute-start(bf16[256,512]{1,0:T(8,128)(2,1)S(1)} %get-tuple-element.10), channel_id=1, source_target_pairs={{0,192},{64,128},{128,64},{192,0},{1,193},{65,129},{129,65},{193,1... | collective-permute-start | bytes 786440 | tf_op jit(solution)/shard_map/ppermute | solution.py:41
  (13 other events, 220.4 us)
where the time goes:
time: 202 us; the launch traced here: 201 us
  waiting for transfers between devices  89.5 us (44%)
  starting transfers between devices  68 us (34%)
  Pallas kernels  13.3 us (7%)
  matrix products  13.3 us (7%)
  other arithmetic  9.34 us (5%)
  local copies, waits for them, and re-layouts  6.31 us (3%)
    ppermute x26, waiting for transfers between devices, swap(): return lax.ppermute(value, axis, [(i, i ^ bit) for i in range(n)])  80.5 us
    ppermute x26, starting transfers between devices, swap(): return lax.ppermute(value, axis, [(i, i ^ bit) for i in range(n)])  43.4 us
    ppermute x4, starting transfers between devices, on_device(): got.append(lax.ppermute(mine, SPREAD, spread_pairs(sizes, k)))  19.9 us
    dot_general x4, matrix products, on_device(): lax.dot_general(g, h, (((0,), (0,)), ((), ())), preferred_element_type=jn...  13.3 us
    pallas_call x2, Pallas kernels, join_grads(): pl.pallas_call(body, out_shape=jax.ShapeDtypeStruct((4 * rows, 4 * width)...  7.82 us
    pallas_call x2, Pallas kernels, join_hidden(): pl.pallas_call(body, out_shape=jax.ShapeDtypeStruct((4 * rows, width), ow...  5.51 us
    ppermute x2, waiting for transfers between devices, on_device(): passed = lax.ppermute(far, 'zl', [(2, 3), (1, 0)])  5.39 us
  transfers between devices with their start and end apart: 34, of which 15 were waited for; matrix products, arithmetic and copies ran while one was open for 9% of the time, Pallas kernels for 5%

commit v1 on v0

--- a/solution.py
+++ b/solution.py
@@ -13,7 +13,6 @@
 CAND = 32
 CAP = 8
 F_CUTS = (512, 384)
-E_CUTS = (256, 256)
 SPREAD = ("zl", "zh", "x", "c")
 SMEM = pl.BlockSpec(memory_space=pltpu.SMEM)
 VMEM = pl.BlockSpec(memory_space=pltpu.VMEM)
@@ -41,31 +40,59 @@
     return lax.ppermute(value, axis, [(i, i ^ bit) for i in range(n)])
 
 
-def grads_body(rows, at_ref, own, rest, c_own, c_rest, out):
-    width = own.shape[2]
-    for s in range(4):
-        for o in range(2):
-            q = (s % 2) * 2 + o
-            for k in range(2):
-                d = (k * 2 + s // 2) ^ at_ref[0]
-                source = (own, c_own)[o].at[k] if s == 0 else (rest, c_rest)[o].at[s - 1, k]
-                columns = pl.ds(pl.multiple_of(d * width, 128), width)
-                out[pl.ds(q * rows, rows), columns] = source[...]
+def copy_rows(source, target, row):
+    rows = source.shape[0]
+    step = 128
+
+    @pl.loop(0, rows // step)
+    def _(i):
+        target[pl.ds(row + i * step, step), :] = source[pl.ds(i * step, step), :]
 
 
-def join_grads(first, own, rest, c_own, c_rest):
-    rows, width = own.shape[1:]
+def join_grads(first, parts):
+    rows, width = parts[0][0][0].shape
+    flat = [a for part in parts for pair in part for a in pair]
+    kind = flat[0].dtype
 
-    def body(*refs):
-        grads_body(rows, *refs)
+    def body(at_ref, *refs):
+        pieces, outs = refs[: len(flat)], refs[len(flat) :]
+        for d in range(4):
+            for block in range(4):
+
+                @pl.when(block ^ at_ref[0] == d)
+                def _(block=block, d=d):
+                    k, high = block // 2, block % 2
+                    for q in range(4):
+                        copy_rows(pieces[k * 8 + (2 * high + q // 2) * 2 + q % 2], outs[d], q * rows)
 
     return pl.pallas_call(
         body,
-        out_shape=jax.ShapeDtypeStruct((4 * rows, 4 * width), own.dtype),
-        in_specs=[SMEM, VMEM, VMEM, VMEM, VMEM],
+        out_shape=[jax.ShapeDtypeStruct((4 * rows, width), kind)] * 4,
+        in_specs=[SMEM] + [VMEM] * len(flat),
+        out_specs=[VMEM] * 4,
+        name="grads",
+        compiler_params=pltpu.CompilerParams(vmem_limit_bytes=16 * 2**20),
+        cost_estimate=pl.CostEstimate(flops=2_000_000_000, bytes_accessed=12_000_000, transcendentals=0),
+    )(first, *flat)
+
+
+def add_up(factor, done, own, got):
+    rows, before = done.shape
+    width = own.shape[1]
+
+    def body(done, own, a, b, c, out):
+        out[:, :before] = done[...]
+        total = own[...] + a[...].astype(jnp.float32) + b[...].astype(jnp.float32) + c[...].astype(jnp.float32)
+        out[:, before:] = (total * factor).astype(out.dtype)
+
+    return pl.pallas_call(
+        body,
+        out_shape=jax.ShapeDtypeStruct((rows, before + width), done.dtype),
+        in_specs=[VMEM] * 5,
         out_specs=VMEM,
-        cost_estimate=pl.CostEstimate(flops=2_000_000_000, bytes_accessed=6_000_000, transcendentals=0),
-    )(first, own, rest, c_own, c_rest)
+        name="add",
+        compiler_params=pltpu.CompilerParams(vmem_limit_bytes=8 * 2**20),
+    )(done, own, *got)
 
 
 def join_hidden(place, own, near, far, middle, passed):
@@ -92,6 +119,7 @@
         out_shape=jax.ShapeDtypeStruct((4 * rows, width), own.dtype),
         in_specs=[SMEM, VMEM, VMEM, VMEM, VMEM, VMEM],
         out_specs=VMEM,
+        compiler_params=pltpu.CompilerParams(vmem_limit_bytes=5 * 2**20),
         cost_estimate=pl.CostEstimate(flops=1_000_000_000, bytes_accessed=3_000_000, transcendentals=0),
     )(place, own, near, far, middle, passed)
 
@@ -107,14 +135,9 @@
     sizes = tuple(lax.axis_size(a) for a in SPREAD)
 
     grads = upstream.reshape(CAND, SEQ, model_part)[picked].reshape(rows, model_part)
-    owns, at = [], 0
-    for width in E_CUTS:
-        mine = grads[:, at : at + width]
-        at += width
-        got = []
-        for k in (0, 1):
-            got.append(lax.ppermute(mine, SPREAD, spread_pairs(sizes, k)))
-        owns.append(jnp.stack(got))
+    owns = []
+    for k in (0, 1):
+        owns.append(lax.ppermute(grads, SPREAD, spread_pairs(sizes, k)))
 
     gate_all = gate_act.reshape(CAND, SEQ, hidden_width)
     up_all = up_act.reshape(CAND, SEQ, hidden_width)
@@ -135,28 +158,26 @@
         hidden_parts.append(join_hidden(place, part, near, far, middle, passed))
 
     first = (((y // 2) ^ zh) * 2 + ((y % 2) ^ (x // 2))).astype(jnp.int32).reshape(1)
-    grad_parts = []
+    parts = []
     for own in owns:
-        c_own = swap(own, "c", 1)
-        rest = jnp.stack([swap(own, "x", s) for s in (1, 2, 3)])
-        c_rest = swap(rest, "c", 1)
-        grad_parts.append(join_grads(first, own, rest, c_own, c_rest))
+        by_x = [own] + [swap(own, "x", s) for s in (1, 2, 3)]
+        parts.append([(a, swap(a, "c", 1)) for a in by_x])
+    blocks = join_grads(first, parts)
 
     factor = 1.0 / math.sqrt(lax.axis_size("y") * lax.axis_size("zl") * CAP * SEQ)
-    columns = []
+    dims = (((0,), (0,)), ((), ()))
+    sums = []
     for h in hidden_parts:
-        pieces = []
-        for g in grad_parts:
-            partial = lax.dot_general(
-                g, h, (((0,), (0,)), ((), ())), preferred_element_type=jnp.float32
-            ).astype(jnp.bfloat16)
-            partial = partial.reshape(4, -1, h.shape[1])
-            total = partial[0].astype(jnp.float32)
-            for d in (1, 3, 2):
-                total = total + swap(partial[d], "y", d).astype(jnp.float32)
-            pieces.append((total * factor).astype(jnp.bfloat16))
-        columns.append(jnp.concatenate(pieces, axis=0))
-    return jnp.concatenate(columns, axis=1)
+        got = []
+        for d in (1, 3, 2, 0):
+            partial = lax.dot_general(blocks[d], h, dims, preferred_element_type=jnp.float32)
+            if d:
+                partial = partial.astype(jnp.bfloat16)
+            got.append(swap(partial, "y", d) if d else partial)
+        sums.append((got[3], got[:3]))
+    own, got = sums[0]
+    done = (own + got[0].astype(jnp.float32) + got[1].astype(jnp.float32) + got[2].astype(jnp.float32)) * factor
+    return add_up(factor, done.astype(jnp.bfloat16), *sums[1])
 
 
 def solution(mesh):

time: 202 us -> 168 us (0.83)
  starting transfers between devices: 68 us -> 45.6 us
  other arithmetic: 9.34 us -> 1.22 us
  local copies, waits for them, and re-layouts: 6.31 us -> 14.1 us
  Pallas kernels: 13.3 us -> 5.84 us
  matrix products: 13.3 us -> 8.16 us
    ppermute x26 -> x24, starting transfers between devices: 43.4 us -> 31.5 us  [swap(): return lax.ppermute(value, axis, [(i, i ^ bit) for i in range(n)])]
    ppermute x4 -> x2, starting transfers between devices: 19.9 us -> 10.2 us  [on_device(): owns.append(lax.ppermute(grads, SPREAD, spread_pairs(sizes, k)))]
    ppermute x26 -> x24, waiting for transfers between devices: 80.5 us -> 90.2 us  [swap(): return lax.ppermute(value, axis, [(i, i ^ bit) for i in range(n)])]
    unnamed x22 -> x36, local copies, waits for them, and re-layouts: 0.04 us -> 7.76 us
    another operation x4 -> x0, other arithmetic: 5.88 us -> none  [the longest x2 3.3 us: on_device(): rest = jnp.stack([swap(own, 'x', s) for s in (1, 2, 3)])]
    dot_general x4 -> x8, matrix products: 13.3 us -> 8.16 us  [on_device(): lax.dot_general(blocks[d], h, dims, preferred_element_type=jnp.float32)]
    ppermute x2, waiting for transfers between devices: 5.39 us -> 0.87 us  [on_device(): passed = lax.ppermute(far, 'zl', [(2, 3), (1, 0)])]
    pallas_call x2, Pallas kernels: 7.82 us -> 3.9 us  [the longest x1 2.73 us: join_grads(): pl.pallas_call(body, out_shape=[jax.ShapeDtypeStruct((4 * rows, width), k...]
  transfers between devices with their start and end apart: 34 -> 30, of which waited for: 15 -> 9; matrix products, arithmetic and copies ran while one was open for 9% -> 5% of each run, Pallas kernels for 5% -> 1%
where the time goes in v1:
time: 168 us; the launch traced here: 167 us
  waiting for transfers between devices  91.1 us (54%)
  starting transfers between devices  45.6 us (27%)
  local copies, waits for them, and re-layouts  14.1 us (8%)
  matrix products  8.16 us (5%)
  Pallas kernels  5.84 us (3%)
    ppermute x24, waiting for transfers between devices, swap(): return lax.ppermute(value, axis, [(i, i ^ bit) for i in range(n)])  90.2 us
    ppermute x24, starting transfers between devices, swap(): return lax.ppermute(value, axis, [(i, i ^ bit) for i in range(n)])  31.5 us
    ppermute x2, starting transfers between devices, on_device(): owns.append(lax.ppermute(grads, SPREAD, spread_pairs(sizes, k)))  10.2 us
    dot_general x8, matrix products, on_device(): lax.dot_general(blocks[d], h, dims, preferred_element_type=jnp.float32)  8.16 us
    unnamed x36, local copies, waits for them, and re-layouts  7.76 us
  transfers between devices with their start and end apart: 30, of which 9 were waited for; matrix products, arithmetic and copies ran while one was open for 5% of the time, Pallas kernels for 1%

profile of v1, /device:TPU:1, one launch (start us, length us, event | category | flops | bytes accessed | tf_op | source)
XLA Modules:
  0.0 167.1 jit_solution(17453338151970829196)
XLA Ops:
  2.3 2.0 %gather_fusion.1 = bf16[16,24,896]{2,1,0:T(8,128)(2,1)S(1)} fusion(bf16[32,24,896]{2,1,0:T(8,128)(2,1)} %bitcast.40, s32[1024]{0:T(1024)S(1)} %pad_clamp_fusion), kind=kCustom, calls=%fused_computation.1 | custom fusion | bytes 1376320 | tf_op jit(solution)/shard_map/gather | solution.py:145
  5.5 5.1 %collective-permute-start.24 = (bf16[384,384]{1,0:T(8,128)(2,1)S(1)}, bf16[384,384]{1,0:T(8,128)(2,1)}, u32[]{:S(2)}, u32[]{:S(2)}) collective-permute-start(bf16[384,384]{1,0:T(8,128)(2,1)S(1)} %slice.15.own), channel_id=1, source_target_pairs={{0,32},{16,48},{32,0},{48,16},{1,33},{17,49},{33,1},{49,17},{2,34}... | collective-permute-start | bytes 884744 | tf_op jit(solution)/shard_map/ppermute | solution.py:40
  11.1 2.4 %gather_fusion = bf16[16,24,512]{2,1,0:T(8,128)(2,1)} fusion(bf16[32,24,512]{2,1,0:T(8,128)(2,1)} %bitcast.41, s32[1024]{0:T(1024)S(1)} %pad_clamp_fusion), kind=kCustom, calls=%fused_computation | custom fusion | bytes 786496 | tf_op jit(solution)/shard_map/gather | solution.py:137
  13.5 5.7 %collective-permute-start.8 = (bf16[384,512]{1,0:T(8,128)(2,1)}, bf16[384,512]{1,0:T(8,128)(2,1)S(1)}, u32[]{:S(2)}, u32[]{:S(2)}) collective-permute-start(bf16[384,512]{1,0:T(8,128)(2,1)} %bitcast.4), channel_id=1, source_target_pairs={{0,8},{1,25},{2,42},{3,59},{4,12},{5,29},{6,46},{7,63},{8,0},{9,17... | collective-permute-start | bytes 1179656 | tf_op jit(solution)/shard_map/ppermute | solution.py:140
  19.2 4.5 %collective-permute-start = (bf16[384,512]{1,0:T(8,128)(2,1)}, bf16[384,512]{1,0:T(8,128)(2,1)S(1)}, u32[]{:S(2)}, u32[]{:S(2)}) collective-permute-start(bf16[384,512]{1,0:T(8,128)(2,1)} %bitcast.4), channel_id=1, source_target_pairs={{0,0},{1,17},{2,34},{3,51},{4,4},{5,21},{6,38},{7,55},{8,8},{9,25}... | collective-permute-start | bytes 1179656 | tf_op jit(solution)/shard_map/ppermute | solution.py:140
  23.7 1.0 slice.14.own
  25.4 29.7 %collective-permute-done.24.far = bf16[384,384]{1,0:T(8,128)(2,1)} collective-permute-done((bf16[384,384]{1,0:T(8,128)(2,1)S(1)}, bf16[384,384]{1,0:T(8,128)(2,1)}, u32[]{:S(2)}, u32[]{:S(2)}) %collective-permute-start.24) | collective-permute-done | bytes 294944 | tf_op jit(solution)/shard_map/ppermute | solution.py:40
  55.2 1.3 collective-permute-start.26
  57.3 2.1 %collective-permute-start.12 = (bf16[384,512]{1,0:T(8,128)(2,1)S(1)}, bf16[384,512]{1,0:T(8,128)(2,1)}, u32[]{:S(2)}, u32[]{:S(2)}) collective-permute-start(bf16[384,512]{1,0:T(8,128)(2,1)S(1)} %collective-permute-done.8.refs_8_), channel_id=1, source_target_pairs={{0,4},{2,6},{4,0},{6,2},{1,5},{3,7},{5,1},{7,3},{8,12},{10,14},{12... | collective-permute-start | bytes 1179656 | tf_op jit(solution)/shard_map/ppermute | solution.py:40
  59.5 20.9 %collective-permute-done.17.far = bf16[384,512]{1,0:T(8,128)(2,1)S(1)} collective-permute-done((bf16[384,512]{1,0:T(8,128)(2,1)S(1)}, bf16[384,512]{1,0:T(8,128)(2,1)S(1)}, u32[]{:S(2)}, u32[]{:S(2)}) %collective-permute-start.17) | collective-permute-done | bytes 393248 | tf_op jit(solution)/shard_map/ppermute | solution.py:40
  81.2 1.4 collective-permute-start.9
  84.2 2.4 %collective-permute-start.6 = (bf16[384,512]{1,0:T(8,128)(2,1)S(1)}, bf16[384,512]{1,0:T(8,128)(2,1)}, u32[]{:S(2)}, u32[]{:S(2)}) collective-permute-start(bf16[384,512]{1,0:T(8,128)(2,1)S(1)} %collective-permute-done.refs_0_), channel_id=1, source_target_pairs={{0,6},{2,4},{4,2},{6,0},{1,7},{3,5},{5,3},{7,1},{8,14},{10,12},{12... | collective-permute-start | bytes 1179656 | tf_op jit(solution)/shard_map/ppermute | solution.py:40
  87.4 2.4 %collective-permute-done.10.refs_10_ = bf16[384,512]{1,0:T(8,128)(2,1)} collective-permute-done((bf16[384,512]{1,0:T(8,128)(2,1)S(1)}, bf16[384,512]{1,0:T(8,128)(2,1)}, u32[]{:S(2)}, u32[]{:S(2)}) %collective-permute-start.10) | collective-permute-done | bytes 393248 | tf_op jit(solution)/shard_map/ppermute | solution.py:40
  89.8 4.1 %collective-permute-start.1 = (bf16[384,512]{1,0:T(8,128)(2,1)S(1)}, bf16[384,512]{1,0:T(8,128)(2,1)S(1)}, u32[]{:S(2)}, u32[]{:S(2)}) collective-permute-start(bf16[384,512]{1,0:T(8,128)(2,1)S(1)} %collective-permute-done.refs_0_), channel_id=1, source_target_pairs={{0,1},{1,0},{2,3},{3,2},{4,5},{5,4},{6,7},{7,6},{8,9},{9,8},{10,11... | collective-permute-start | bytes 1179656 | tf_op jit(solution)/shard_map/ppermute | solution.py:40
  94.7 1.3 collective-permute-start.19
  96.7 6.8 %collective-permute-done.6.refs_6_ = bf16[384,512]{1,0:T(8,128)(2,1)} collective-permute-done((bf16[384,512]{1,0:T(8,128)(2,1)S(1)}, bf16[384,512]{1,0:T(8,128)(2,1)}, u32[]{:S(2)}, u32[]{:S(2)}) %collective-permute-start.6) | collective-permute-done | bytes 393248 | tf_op jit(solution)/shard_map/ppermute | solution.py:40
  103.5 1.9 %collective-permute-start.15 = (bf16[384,512]{1,0:T(8,128)(2,1)S(1)}, bf16[384,512]{1,0:T(8,128)(2,1)S(1)}, u32[]{:S(2)}, u32[]{:S(2)}) collective-permute-start(bf16[384,512]{1,0:T(8,128)(2,1)S(1)} %collective-permute-done.14.refs_14_), channel_id=1, source_target_pairs={{0,1},{1,0},{2,3},{3,2},{4,5},{5,4},{6,7},{7,6},{8,9},{9,8},{10,11... | collective-permute-start | bytes 1179656 | tf_op jit(solution)/shard_map/ppermute | solution.py:40
  106.7 2.3 %collective-permute-start.11 = (bf16[384,512]{1,0:T(8,128)(2,1)}, bf16[384,512]{1,0:T(8,128)(2,1)}, u32[]{:S(2)}, u32[]{:S(2)}) collective-permute-start(bf16[384,512]{1,0:T(8,128)(2,1)} %collective-permute-done.10.refs_10_), channel_id=1, source_target_pairs={{0,1},{1,0},{2,3},{3,2},{4,5},{5,4},{6,7},{7,6},{8,9},{9,8},{10,11... | collective-permute-start | bytes 1179656 | tf_op jit(solution)/shard_map/ppermute | solution.py:40
  112.8 1.3 shard_map.56
  115.5 2.7 %grads.1 = (bf16[1536,512]{1,0:T(8,128)(2,1)S(1)}, bf16[1536,512]{1,0:T(8,128)(2,1)S(1)}, bf16[1536,512]{1,0:T(8,128)(2,1)S(1)}, bf16[1536,512]{1,0:T(8,128)(2,1)S(1)}) custom-call(s32[1]{0:T(128)} %bitcast.at_ref, bf16[384,512]{1,0:T(8,128)(2,1)S(1)} %collective-permute-done.refs_0_, bf16[384,512]{1,0:T(8,128)(2,1)S(1)} %copy-done.10, ...), custom_call_target="tpu_custom_call" | custom-call | flops 2000000000 | bytes 12000000 | tf_op jit(solution)/shard_map/grads/pallas_call | solution.py:68
  118.3 1.0 convolution_convert_fusion.4
  119.3 1.0 convolution_convert_fusion.5
  122.3 1.4 collective-permute-start.27
  123.7 1.9 %collective-permute-start.28 = (bf16[512,384]{1,0:T(8,128)(2,1)S(1)}, bf16[512,384]{1,0:T(8,128)(2,1)S(1)}, u32[]{:S(2)}, u32[]{:S(2)}) collective-permute-start(bf16[512,384]{1,0:T(8,128)(2,1)S(1)} %convolution_convert_fusion.4), channel_id=1, source_target_pairs={{0,192},{64,128},{128,64},{192,0},{1,193},{65,129},{129,65},{193,1... | collective-permute-start | bytes 1179656 | tf_op jit(solution)/shard_map/ppermute | solution.py:40
  127.7 2.3 %collective-permute-start.22 = (bf16[512,512]{1,0:T(8,128)(2,1)S(1)}, bf16[512,512]{1,0:T(8,128)(2,1)S(1)}, u32[]{:S(2)}, u32[]{:S(2)}) collective-permute-start(bf16[512,512]{1,0:T(8,128)(2,1)S(1)} %convolution_convert_fusion), channel_id=1, source_target_pairs={{0,128},{64,192},{128,0},{192,64},{1,129},{65,193},{129,1},{193,65... | collective-permute-start | bytes 1572872 | tf_op jit(solution)/shard_map/ppermute | solution.py:40
  130.0 1.0 convolution_convert_fusion.3
  131.0 1.0 fusion.11.own
  132.0 11.8 %collective-permute-done.20 = bf16[512,512]{1,0:T(8,128)(2,1)S(1)} collective-permute-done((bf16[512,512]{1,0:T(8,128)(2,1)S(1)}, bf16[512,512]{1,0:T(8,128)(2,1)S(1)}, u32[]{:S(2)}, u32[]{:S(2)}) %collective-permute-start.20) | collective-permute-done | bytes 524320 | tf_op jit(solution)/shard_map/ppermute | solution.py:40
  143.8 2.9 %collective-permute-start.29 = (bf16[512,384]{1,0:T(8,128)(2,1)S(1)}, bf16[512,384]{1,0:T(8,128)(2,1)S(1)}, u32[]{:S(2)}, u32[]{:S(2)}) collective-permute-start(bf16[512,384]{1,0:T(8,128)(2,1)S(1)} %convolution_convert_fusion.3), channel_id=1, source_target_pairs={{0,128},{64,192},{128,0},{192,64},{1,129},{65,193},{129,1},{193,65... | collective-permute-start | bytes 1179656 | tf_op jit(solution)/shard_map/ppermute | solution.py:40
  146.7 17.3 %collective-permute-done.21 = bf16[512,512]{1,0:T(8,128)(2,1)S(1)} collective-permute-done((bf16[512,512]{1,0:T(8,128)(2,1)S(1)}, bf16[512,512]{1,0:T(8,128)(2,1)S(1)}, u32[]{:S(2)}, u32[]{:S(2)}) %collective-permute-start.21) | collective-permute-done | bytes 524320 | tf_op jit(solution)/shard_map/ppermute | solution.py:40
  164.1 1.1 fusion.8.done
  165.9 1.2 add.88
  (88 shorter events, 20.6 us)
Async XLA Ops:
  0.0 1.6 copy-start
  4.8 8.7 %copy-start.17 = (bf16[384,896]{1,0:T(8,128)(2,1)}, bf16[384,896]{1,0:T(8,128)(2,1)S(1)}, u32[]{:S(2)}) copy-start(bf16[384,896]{1,0:T(8,128)(2,1)S(1)} %fusion.9) | copy-start | bytes 2064388
  4.8 19.9 %collective-permute-start.25 = (bf16[384,384]{1,0:T(8,128)(2,1)S(1)}, bf16[384,384]{1,0:T(8,128)(2,1)S(1)}, u32[]{:S(2)}, u32[]{:S(2)}) collective-permute-start(bf16[384,384]{1,0:T(8,128)(2,1)S(1)} %slice.15.own), channel_id=1, source_target_pairs={{16,32},{32,16},{17,33},{33,17},{18,34},{34,18},{19,35},{35,19},{2... | collective-permute-start | bytes 884744 | tf_op jit(solution)/shard_map/ppermute | solution.py:156
  5.5 49.7 %collective-permute-start.24 = (bf16[384,384]{1,0:T(8,128)(2,1)S(1)}, bf16[384,384]{1,0:T(8,128)(2,1)}, u32[]{:S(2)}, u32[]{:S(2)}) collective-permute-start(bf16[384,384]{1,0:T(8,128)(2,1)S(1)} %slice.15.own), channel_id=1, source_target_pairs={{0,32},{16,48},{32,0},{48,16},{1,33},{17,49},{33,1},{49,17},{2,34}... | collective-permute-start | bytes 884744 | tf_op jit(solution)/shard_map/ppermute | solution.py:40
  10.7 44.5 %collective-permute-start.23 = (bf16[384,384]{1,0:T(8,128)(2,1)S(1)}, bf16[384,384]{1,0:T(8,128)(2,1)}, u32[]{:S(2)}, u32[]{:S(2)}) collective-permute-start(bf16[384,384]{1,0:T(8,128)(2,1)S(1)} %slice.15.own), channel_id=1, source_target_pairs={{0,16},{16,0},{32,48},{48,32},{1,17},{17,1},{33,49},{49,33},{2,18}... | collective-permute-start | bytes 884744 | tf_op jit(solution)/shard_map/ppermute | solution.py:40
  13.5 41.7 %collective-permute-start.8 = (bf16[384,512]{1,0:T(8,128)(2,1)}, bf16[384,512]{1,0:T(8,128)(2,1)S(1)}, u32[]{:S(2)}, u32[]{:S(2)}) collective-permute-start(bf16[384,512]{1,0:T(8,128)(2,1)} %bitcast.4), channel_id=1, source_target_pairs={{0,8},{1,25},{2,42},{3,59},{4,12},{5,29},{6,46},{7,63},{8,0},{9,17... | collective-permute-start | bytes 1179656 | tf_op jit(solution)/shard_map/ppermute | solution.py:140
  19.2 37.3 %collective-permute-start = (bf16[384,512]{1,0:T(8,128)(2,1)}, bf16[384,512]{1,0:T(8,128)(2,1)S(1)}, u32[]{:S(2)}, u32[]{:S(2)}) collective-permute-start(bf16[384,512]{1,0:T(8,128)(2,1)} %bitcast.4), channel_id=1, source_target_pairs={{0,0},{1,17},{2,34},{3,51},{4,4},{5,21},{6,38},{7,55},{8,8},{9,25}... | collective-permute-start | bytes 1179656 | tf_op jit(solution)/shard_map/ppermute | solution.py:140
  24.7 32.6 %collective-permute-start.18 = (bf16[384,512]{1,0:T(8,128)(2,1)S(1)}, bf16[384,512]{1,0:T(8,128)(2,1)S(1)}, u32[]{:S(2)}, u32[]{:S(2)}) collective-permute-start(bf16[384,512]{1,0:T(8,128)(2,1)S(1)} %slice.14.own), channel_id=1, source_target_pairs={{16,32},{32,16},{17,33},{33,17},{18,34},{34,18},{19,35},{35,19},{2... | collective-permute-start | bytes 1179656 | tf_op jit(solution)/shard_map/ppermute | solution.py:156
  55.2 25.2 %collective-permute-start.17 = (bf16[384,512]{1,0:T(8,128)(2,1)S(1)}, bf16[384,512]{1,0:T(8,128)(2,1)S(1)}, u32[]{:S(2)}, u32[]{:S(2)}) collective-permute-start(bf16[384,512]{1,0:T(8,128)(2,1)S(1)} %slice.14.own), channel_id=1, source_target_pairs={{0,32},{16,48},{32,0},{48,16},{1,33},{17,49},{33,1},{49,17},{2,34}... | collective-permute-start | bytes 1179656 | tf_op jit(solution)/shard_map/ppermute | solution.py:40
  55.2 25.2 %collective-permute-start.16 = (bf16[384,512]{1,0:T(8,128)(2,1)S(1)}, bf16[384,512]{1,0:T(8,128)(2,1)S(1)}, u32[]{:S(2)}, u32[]{:S(2)}) collective-permute-start(bf16[384,512]{1,0:T(8,128)(2,1)S(1)} %slice.14.own), channel_id=1, source_target_pairs={{0,16},{16,0},{32,48},{48,32},{1,17},{17,1},{33,49},{49,33},{2,18}... | collective-permute-start | bytes 1179656 | tf_op jit(solution)/shard_map/ppermute | solution.py:40
  55.2 28.2 %collective-permute-start.26 = (bf16[384,384]{1,0:T(8,128)(2,1)}, bf16[384,384]{1,0:T(8,128)(2,1)S(1)}, u32[]{:S(2)}, u32[]{:S(2)}) collective-permute-start(bf16[384,384]{1,0:T(8,128)(2,1)} %collective-permute-done.24.far), channel_id=1, source_target_pairs={{32,48},{16,0},{33,49},{17,1},{34,50},{18,2},{35,51},{19,3},{36,52... | collective-permute-start | bytes 884744 | tf_op jit(solution)/shard_map/ppermute | solution.py:157
  56.5 30.1 %collective-permute-start.14 = (bf16[384,512]{1,0:T(8,128)(2,1)S(1)}, bf16[384,512]{1,0:T(8,128)(2,1)S(1)}, u32[]{:S(2)}, u32[]{:S(2)}) collective-permute-start(bf16[384,512]{1,0:T(8,128)(2,1)S(1)} %collective-permute-done.8.refs_8_), channel_id=1, source_target_pairs={{0,6},{2,4},{4,2},{6,0},{1,7},{3,5},{5,3},{7,1},{8,14},{10,12},{12... | collective-permute-start | bytes 1179656 | tf_op jit(solution)/shard_map/ppermute | solution.py:40
  57.3 29.6 %collective-permute-start.12 = (bf16[384,512]{1,0:T(8,128)(2,1)S(1)}, bf16[384,512]{1,0:T(8,128)(2,1)}, u32[]{:S(2)}, u32[]{:S(2)}) collective-permute-start(bf16[384,512]{1,0:T(8,128)(2,1)S(1)} %collective-permute-done.8.refs_8_), channel_id=1, source_target_pairs={{0,4},{2,6},{4,0},{6,2},{1,5},{3,7},{5,1},{7,3},{8,12},{10,14},{12... | collective-permute-start | bytes 1179656 | tf_op jit(solution)/shard_map/ppermute | solution.py:40
  80.4 9.4 %collective-permute-start.10 = (bf16[384,512]{1,0:T(8,128)(2,1)S(1)}, bf16[384,512]{1,0:T(8,128)(2,1)}, u32[]{:S(2)}, u32[]{:S(2)}) collective-permute-start(bf16[384,512]{1,0:T(8,128)(2,1)S(1)} %collective-permute-done.8.refs_8_), channel_id=1, source_target_pairs={{0,2},{2,0},{4,6},{6,4},{1,3},{3,1},{5,7},{7,5},{8,10},{10,8},{12,... | collective-permute-start | bytes 1179656 | tf_op jit(solution)/shard_map/ppermute | solution.py:40
  81.2 12.7 %collective-permute-start.9 = (bf16[384,512]{1,0:T(8,128)(2,1)S(1)}, bf16[384,512]{1,0:T(8,128)(2,1)S(1)}, u32[]{:S(2)}, u32[]{:S(2)}) collective-permute-start(bf16[384,512]{1,0:T(8,128)(2,1)S(1)} %collective-permute-done.8.refs_8_), channel_id=1, source_target_pairs={{0,1},{1,0},{2,3},{3,2},{4,5},{5,4},{6,7},{7,6},{8,9},{9,8},{10,11... | collective-permute-start | bytes 1179656 | tf_op jit(solution)/shard_map/ppermute | solution.py:40
  84.2 19.3 %collective-permute-start.6 = (bf16[384,512]{1,0:T(8,128)(2,1)S(1)}, bf16[384,512]{1,0:T(8,128)(2,1)}, u32[]{:S(2)}, u32[]{:S(2)}) collective-permute-start(bf16[384,512]{1,0:T(8,128)(2,1)S(1)} %collective-permute-done.refs_0_), channel_id=1, source_target_pairs={{0,6},{2,4},{4,2},{6,0},{1,7},{3,5},{5,3},{7,1},{8,14},{10,12},{12... | collective-permute-start | bytes 1179656 | tf_op jit(solution)/shard_map/ppermute | solution.py:40
  86.6 19.6 %collective-permute-start.4 = (bf16[384,512]{1,0:T(8,128)(2,1)S(1)}, bf16[384,512]{1,0:T(8,128)(2,1)}, u32[]{:S(2)}, u32[]{:S(2)}) collective-permute-start(bf16[384,512]{1,0:T(8,128)(2,1)S(1)} %collective-permute-done.refs_0_), channel_id=1, source_target_pairs={{0,4},{2,6},{4,0},{6,2},{1,5},{3,7},{5,1},{7,3},{8,12},{10,14},{12... | collective-permute-start | bytes 1179656 | tf_op jit(solution)/shard_map/ppermute | solution.py:40
  86.9 19.8 %collective-permute-start.2 = (bf16[384,512]{1,0:T(8,128)(2,1)S(1)}, bf16[384,512]{1,0:T(8,128)(2,1)}, u32[]{:S(2)}, u32[]{:S(2)}) collective-permute-start(bf16[384,512]{1,0:T(8,128)(2,1)S(1)} %collective-permute-done.refs_0_), channel_id=1, source_target_pairs={{0,2},{2,0},{4,6},{6,4},{1,3},{3,1},{5,7},{7,5},{8,10},{10,8},{12,... | collective-permute-start | bytes 1179656 | tf_op jit(solution)/shard_map/ppermute | solution.py:40
  89.8 19.2 %collective-permute-start.1 = (bf16[384,512]{1,0:T(8,128)(2,1)S(1)}, bf16[384,512]{1,0:T(8,128)(2,1)S(1)}, u32[]{:S(2)}, u32[]{:S(2)}) collective-permute-start(bf16[384,512]{1,0:T(8,128)(2,1)S(1)} %collective-permute-done.refs_0_), channel_id=1, source_target_pairs={{0,1},{1,0},{2,3},{3,2},{4,5},{5,4},{6,7},{7,6},{8,9},{9,8},{10,11... | collective-permute-start | bytes 1179656 | tf_op jit(solution)/shard_map/ppermute | solution.py:40
  94.7 15.0 %collective-permute-start.19 = (bf16[384,512]{1,0:T(8,128)(2,1)S(1)}, bf16[384,512]{1,0:T(8,128)(2,1)S(1)}, u32[]{:S(2)}, u32[]{:S(2)}) collective-permute-start(bf16[384,512]{1,0:T(8,128)(2,1)S(1)} %collective-permute-done.17.far), channel_id=1, source_target_pairs={{32,48},{16,0},{33,49},{17,1},{34,50},{18,2},{35,51},{19,3},{36,52... | collective-permute-start | bytes 1179656 | tf_op jit(solution)/shard_map/ppermute | solution.py:157
  103.5 7.5 %collective-permute-start.15 = (bf16[384,512]{1,0:T(8,128)(2,1)S(1)}, bf16[384,512]{1,0:T(8,128)(2,1)S(1)}, u32[]{:S(2)}, u32[]{:S(2)}) collective-permute-start(bf16[384,512]{1,0:T(8,128)(2,1)S(1)} %collective-permute-done.14.refs_14_), channel_id=1, source_target_pairs={{0,1},{1,0},{2,3},{3,2},{4,5},{5,4},{6,7},{7,6},{8,9},{9,8},{10,11... | collective-permute-start | bytes 1179656 | tf_op jit(solution)/shard_map/ppermute | solution.py:40
  106.2 8.6 %collective-permute-start.13 = (bf16[384,512]{1,0:T(8,128)(2,1)}, bf16[384,512]{1,0:T(8,128)(2,1)}, u32[]{:S(2)}, u32[]{:S(2)}) collective-permute-start(bf16[384,512]{1,0:T(8,128)(2,1)} %collective-permute-done.12.refs_12_), channel_id=1, source_target_pairs={{0,1},{1,0},{2,3},{3,2},{4,5},{5,4},{6,7},{7,6},{8,9},{9,8},{10,11... | collective-permute-start | bytes 1179656 | tf_op jit(solution)/shard_map/ppermute | solution.py:40
  106.7 8.2 %collective-permute-start.11 = (bf16[384,512]{1,0:T(8,128)(2,1)}, bf16[384,512]{1,0:T(8,128)(2,1)}, u32[]{:S(2)}, u32[]{:S(2)}) collective-permute-start(bf16[384,512]{1,0:T(8,128)(2,1)} %collective-permute-done.10.refs_10_), channel_id=1, source_target_pairs={{0,1},{1,0},{2,3},{3,2},{4,5},{5,4},{6,7},{7,6},{8,9},{9,8},{10,11... | collective-permute-start | bytes 1179656 | tf_op jit(solution)/shard_map/ppermute | solution.py:40
  109.7 5.2 %collective-permute-start.7 = (bf16[384,512]{1,0:T(8,128)(2,1)}, bf16[384,512]{1,0:T(8,128)(2,1)}, u32[]{:S(2)}, u32[]{:S(2)}) collective-permute-start(bf16[384,512]{1,0:T(8,128)(2,1)} %collective-permute-done.6.refs_6_), channel_id=1, source_target_pairs={{0,1},{1,0},{2,3},{3,2},{4,5},{5,4},{6,7},{7,6},{8,9},{9,8},{10,11... | collective-permute-start | bytes 1179656 | tf_op jit(solution)/shard_map/ppermute | solution.py:40
  110.5 4.4 %collective-permute-start.5 = (bf16[384,512]{1,0:T(8,128)(2,1)}, bf16[384,512]{1,0:T(8,128)(2,1)}, u32[]{:S(2)}, u32[]{:S(2)}) collective-permute-start(bf16[384,512]{1,0:T(8,128)(2,1)} %collective-permute-done.4.refs_4_), channel_id=1, source_target_pairs={{0,1},{1,0},{2,3},{3,2},{4,5},{5,4},{6,7},{7,6},{8,9},{9,8},{10,11... | collective-permute-start | bytes 1179656 | tf_op jit(solution)/shard_map/ppermute | solution.py:40
  111.7 3.2 %collective-permute-start.3 = (bf16[384,512]{1,0:T(8,128)(2,1)}, bf16[384,512]{1,0:T(8,128)(2,1)}, u32[]{:S(2)}, u32[]{:S(2)}) collective-permute-start(bf16[384,512]{1,0:T(8,128)(2,1)} %collective-permute-done.2.refs_2_), channel_id=1, source_target_pairs={{0,1},{1,0},{2,3},{3,2},{4,5},{5,4},{6,7},{7,6},{8,9},{9,8},{10,11... | collective-permute-start | bytes 1179656 | tf_op jit(solution)/shard_map/ppermute | solution.py:40
  122.3 42.9 %collective-permute-start.27 = (bf16[512,384]{1,0:T(8,128)(2,1)S(1)}, bf16[512,384]{1,0:T(8,128)(2,1)S(1)}, u32[]{:S(2)}, u32[]{:S(2)}) collective-permute-start(bf16[512,384]{1,0:T(8,128)(2,1)S(1)} %convolution_convert_fusion.5), channel_id=1, source_target_pairs={{0,64},{64,0},{128,192},{192,128},{1,65},{65,1},{129,193},{193,129... | collective-permute-start | bytes 1179656 | tf_op jit(solution)/shard_map/ppermute | solution.py:40
  123.7 41.5 %collective-permute-start.28 = (bf16[512,384]{1,0:T(8,128)(2,1)S(1)}, bf16[512,384]{1,0:T(8,128)(2,1)S(1)}, u32[]{:S(2)}, u32[]{:S(2)}) collective-permute-start(bf16[512,384]{1,0:T(8,128)(2,1)S(1)} %convolution_convert_fusion.4), channel_id=1, source_target_pairs={{0,192},{64,128},{128,64},{192,0},{1,193},{65,129},{129,65},{193,1... | collective-permute-start | bytes 1179656 | tf_op jit(solution)/shard_map/ppermute | solution.py:40
  126.6 17.2 %collective-permute-start.20 = (bf16[512,512]{1,0:T(8,128)(2,1)S(1)}, bf16[512,512]{1,0:T(8,128)(2,1)S(1)}, u32[]{:S(2)}, u32[]{:S(2)}) collective-permute-start(bf16[512,512]{1,0:T(8,128)(2,1)S(1)} %convolution_convert_fusion.2), channel_id=1, source_target_pairs={{0,64},{64,0},{128,192},{192,128},{1,65},{65,1},{129,193},{193,129... | collective-permute-start | bytes 1572872 | tf_op jit(solution)/shard_map/ppermute | solution.py:40
  127.1 37.0 %collective-permute-start.21 = (bf16[512,512]{1,0:T(8,128)(2,1)S(1)}, bf16[512,512]{1,0:T(8,128)(2,1)S(1)}, u32[]{:S(2)}, u32[]{:S(2)}) collective-permute-start(bf16[512,512]{1,0:T(8,128)(2,1)S(1)} %convolution_convert_fusion.1), channel_id=1, source_target_pairs={{0,192},{64,128},{128,64},{192,0},{1,193},{65,129},{129,65},{193,1... | collective-permute-start | bytes 1572872 | tf_op jit(solution)/shard_map/ppermute | solution.py:40
  127.7 36.4 %collective-permute-start.22 = (bf16[512,512]{1,0:T(8,128)(2,1)S(1)}, bf16[512,512]{1,0:T(8,128)(2,1)S(1)}, u32[]{:S(2)}, u32[]{:S(2)}) collective-permute-start(bf16[512,512]{1,0:T(8,128)(2,1)S(1)} %convolution_convert_fusion), channel_id=1, source_target_pairs={{0,128},{64,192},{128,0},{192,64},{1,129},{65,193},{129,1},{193,65... | collective-permute-start | bytes 1572872 | tf_op jit(solution)/shard_map/ppermute | solution.py:40
  143.8 22.1 %collective-permute-start.29 = (bf16[512,384]{1,0:T(8,128)(2,1)S(1)}, bf16[512,384]{1,0:T(8,128)(2,1)S(1)}, u32[]{:S(2)}, u32[]{:S(2)}) collective-permute-start(bf16[512,384]{1,0:T(8,128)(2,1)S(1)} %convolution_convert_fusion.3), channel_id=1, source_target_pairs={{0,128},{64,192},{128,0},{192,64},{1,129},{65,193},{129,1},{193,65... | collective-permute-start | bytes 1179656 | tf_op jit(solution)/shard_map/ppermute | solution.py:40
  (16 other events, 15.7 us)

commit v2 on v1

--- a/solution.py
+++ b/solution.py
@@ -18,7 +18,7 @@
 VMEM = pl.BlockSpec(memory_space=pltpu.VMEM)
 
 
-def spread_pairs(sizes, flip):
+def spread_pairs(sizes, flip, moved):
     zl, zh, x, c = sizes
 
     def at(a, b, d, e):
@@ -29,7 +29,7 @@
         for h in range(zh):
             for i in range(x):
                 for k in range(c):
-                    z_to = (i % 2) * 2 + k
+                    z_to = ((i ^ moved) % 2) * 2 + k
                     r = z_to ^ z_from
                     pairs.append((at(z_from, h, i, k), at(z_to, h ^ flip, (i // 2) * 2 + r // 2, r % 2)))
     return pairs
@@ -42,7 +42,7 @@
 
 def copy_rows(source, target, row):
     rows = source.shape[0]
-    step = 128
+    step = 192
 
     @pl.loop(0, rows // step)
     def _(i):
@@ -50,9 +50,10 @@
 
 
 def join_grads(first, parts):
-    rows, width = parts[0][0][0].shape
+    rows, width = parts[0][0][0].shape[1:]
     flat = [a for part in parts for pair in part for a in pair]
     kind = flat[0].dtype
+    whole = rows * len(parts)
 
     def body(at_ref, *refs):
         pieces, outs = refs[: len(flat)], refs[len(flat) :]
@@ -62,12 +63,14 @@
                 @pl.when(block ^ at_ref[0] == d)
                 def _(block=block, d=d):
                     k, high = block // 2, block % 2
-                    for q in range(4):
-                        copy_rows(pieces[k * 8 + (2 * high + q // 2) * 2 + q % 2], outs[d], q * rows)
+                    for h in range(len(parts)):
+                        for q in range(4):
+                            piece = pieces[h * 8 + (2 * high + q // 2) * 2 + q % 2]
+                            copy_rows(piece.at[k], outs[d], q * whole + h * rows)
 
     return pl.pallas_call(
         body,
-        out_shape=[jax.ShapeDtypeStruct((4 * rows, width), kind)] * 4,
+        out_shape=[jax.ShapeDtypeStruct((4 * whole, width), kind)] * 4,
         in_specs=[SMEM] + [VMEM] * len(flat),
         out_specs=[VMEM] * 4,
         name="grads",
@@ -135,9 +138,13 @@
     sizes = tuple(lax.axis_size(a) for a in SPREAD)
 
     grads = upstream.reshape(CAND, SEQ, model_part)[picked].reshape(rows, model_part)
+    half = rows // 2
     owns = []
-    for k in (0, 1):
-        owns.append(lax.ppermute(grads, SPREAD, spread_pairs(sizes, k)))
+    for h, mine in enumerate((grads[:half], swap(grads[half:], "x", 1))):
+        got = []
+        for k in (0, 1):
+            got.append(lax.ppermute(mine, SPREAD, spread_pairs(sizes, k, h)))
+        owns.append(jnp.stack(got))
 
     gate_all = gate_act.reshape(CAND, SEQ, hidden_width)
     up_all = up_act.reshape(CAND, SEQ, hidden_width)
@@ -160,7 +167,9 @@
     first = (((y // 2) ^ zh) * 2 + ((y % 2) ^ (x // 2))).astype(jnp.int32).reshape(1)
     parts = []
     for own in owns:
-        by_x = [own] + [swap(own, "x", s) for s in (1, 2, 3)]
+        one, three = (swap(own, "x", s) for s in (1, 3))
+        two = jnp.stack([swap(one[0], "x", 3), swap(three[1], "x", 1)])
+        by_x = [own, one, two, three]
         parts.append([(a, swap(a, "c", 1)) for a in by_x])
     blocks = join_grads(first, parts)
 
@@ -169,7 +178,7 @@
     sums = []
     for h in hidden_parts:
         got = []
-        for d in (1, 3, 2, 0):
+        for d in (2, 1, 3, 0):
             partial = lax.dot_general(blocks[d], h, dims, preferred_element_type=jnp.float32)
             if d:
                 partial = partial.astype(jnp.bfloat16)

time: 168 us -> 177 us (1.054)
  starting transfers between devices: 45.6 us -> 74.7 us
  waiting for transfers between devices: 91.1 us -> 65.8 us
  local copies, waits for them, and re-layouts: 14.1 us -> 19.4 us
    ppermute x24 -> x27, waiting for transfers between devices: 90.2 us -> 50.3 us  [swap(): return lax.ppermute(value, axis, [(i, i ^ bit) for i in range(n)])]
    ppermute x24 -> x27, starting transfers between devices: 31.5 us -> 50.4 us  [swap(): return lax.ppermute(value, axis, [(i, i ^ bit) for i in range(n)])]
    ppermute x2, waiting for transfers between devices: 0.87 us -> 11.9 us  [on_device(): passed = lax.ppermute(far, 'zl', [(2, 3), (1, 0)])]
    ppermute x2 -> x4, starting transfers between devices: 10.2 us -> 20.4 us  [on_device(): got.append(lax.ppermute(mine, SPREAD, spread_pairs(sizes, k, h)))]
    ppermute x2 -> x4, waiting for transfers between devices: 0.01 us -> 3.55 us  [on_device(): got.append(lax.ppermute(mine, SPREAD, spread_pairs(sizes, k, h)))]
    unnamed x36 -> x54, local copies, waits for them, and re-layouts: 7.76 us -> 11.3 us
    squeeze x0 -> x4, local copies, waits for them, and re-layouts: none -> 2.83 us  [on_device(): two = jnp.stack([swap(one[0], 'x', 3), swap(three[1], 'x', 1)])]
  transfers between devices with their start and end apart: 30 -> 35, of which waited for: 9 -> 9; matrix products, arithmetic and copies ran while one was open for 5% -> 7% of each run, Pallas kernels for 1% -> 1%
where the time goes in v2:
time: 177 us
  starting transfers between devices  74.7 us (42%)
  waiting for transfers between devices  65.8 us (37%)
  local copies, waits for them, and re-layouts  19.4 us (11%)
  matrix products  8.16 us (5%)
  Pallas kernels  4.84 us (3%)
  other arithmetic  2.5 us (1%)
    ppermute x27, starting transfers between devices, swap(): return lax.ppermute(value, axis, [(i, i ^ bit) for i in range(n)])  50.4 us
    ppermute x27, waiting for transfers between devices, swap(): return lax.ppermute(value, axis, [(i, i ^ bit) for i in range(n)])  50.3 us
    ppermute x4, starting transfers between devices, on_device(): got.append(lax.ppermute(mine, SPREAD, spread_pairs(sizes, k, h)))  20.4 us
    ppermute x2, waiting for transfers between devices, on_device(): passed = lax.ppermute(far, 'zl', [(2, 3), (1, 0)])  11.9 us
    unnamed x54, local copies, waits for them, and re-layouts  11.3 us
    dot_general x8, matrix products, on_device(): lax.dot_general(blocks[d], h, dims, preferred_element_type=jnp.float32)  8.16 us
    ppermute x4, waiting for transfers between devices, on_device(): got.append(lax.ppermute(mine, SPREAD, spread_pairs(sizes, k, h)))  3.55 us
  transfers between devices with their start and end apart: 35, of which 9 were waited for; matrix products, arithmetic and copies ran while one was open for 7% of the time, Pallas kernels for 1%

profile of v2, /device:TPU:1, one launch (start us, length us, event | category | flops | bytes accessed | tf_op | source)
XLA Modules:
  0.0 176.6 jit_solution(15458303759092226482)
XLA Ops:
  0.8 1.7 gather_fusion
  3.2 7.3 %collective-permute-start.1 = (bf16[192,512]{1,0:T(8,128)(2,1)}, bf16[192,512]{1,0:T(8,128)(2,1)}, u32[]{:S(2)}, u32[]{:S(2)}) collective-permute-start(bf16[192,512]{1,0:T(8,128)(2,1)} %bitcast.4), channel_id=1, source_target_pairs={{0,8},{1,25},{2,42},{3,59},{4,12},{5,29},{6,46},{7,63},{8,0},{9,17... | collective-permute-start | bytes 589832 | tf_op jit(solution)/shard_map/ppermute | solution.py:146
  10.5 3.6 %collective-permute-start = (bf16[192,512]{1,0:T(8,128)(2,1)}, bf16[192,512]{1,0:T(8,128)(2,1)}, u32[]{:S(2)}, u32[]{:S(2)}) collective-permute-start(bf16[192,512]{1,0:T(8,128)(2,1)} %bitcast.4), channel_id=1, source_target_pairs={{0,0},{1,17},{2,34},{3,51},{4,4},{5,21},{6,38},{7,55},{8,8},{9,25}... | collective-permute-start | bytes 589832 | tf_op jit(solution)/shard_map/ppermute | solution.py:146
  14.1 2.2 %collective-permute-start.10 = (bf16[192,512]{1,0:T(8,128)(2,1)S(1)}, bf16[192,512]{1,0:T(8,128)(2,1)}, u32[]{:S(2)}, u32[]{:S(2)}) collective-permute-start(bf16[192,512]{1,0:T(8,128)(2,1)S(1)} %bitcast.63), channel_id=1, source_target_pairs={{0,2},{2,0},{4,6},{6,4},{1,3},{3,1},{5,7},{7,5},{8,10},{10,8},{12,... | collective-permute-start | bytes 589832 | tf_op jit(solution)/shard_map/ppermute | solution.py:40
  17.8 2.0 %gather_fusion.1 = bf16[16,24,896]{2,1,0:T(8,128)(2,1)S(1)} fusion(bf16[32,24,896]{2,1,0:T(8,128)(2,1)} %bitcast.57, s32[1024]{0:T(1024)S(1)} %pad_clamp_fusion), kind=kCustom, calls=%fused_computation.1 | custom fusion | bytes 1376320 | tf_op jit(solution)/shard_map/gather | solution.py:152
  19.9 1.1 pad_maximum_fusion.refs_0_
  20.9 7.3 %collective-permute-start.6 = (bf16[2,192,512]{2,1,0:T(8,128)(2,1)S(1)}, bf16[2,192,512]{2,1,0:T(8,128)(2,1)S(1)}, u32[]{:S(2)}, u32[]{:S(2)}) collective-permute-start(bf16[2,192,512]{2,1,0:T(8,128)(2,1)S(1)} %pad_maximum_fusion.refs_0_), channel_id=1, source_target_pairs={{0,6},{2,4},{4,2},{6,0},{1,7},{3,5},{5,3},{7,1},{8,14},{10,12},{12... | collective-permute-start | bytes 1179656 | tf_op jit(solution)/shard_map/ppermute | solution.py:40
  28.8 1.6 collective-permute-start.12
  30.4 7.9 %collective-permute-start.11 = (bf16[192,512]{1,0:T(8,128)(2,1)}, bf16[192,512]{1,0:T(8,128)(2,1)S(1)}, u32[]{:S(2)}, u32[]{:S(2)}) collective-permute-start(bf16[192,512]{1,0:T(8,128)(2,1)} %collective-permute-done.10), channel_id=1, source_target_pairs={{0,34},{1,51},{2,0},{3,17},{4,38},{5,55},{6,4},{7,21},{8,42},{9,59... | collective-permute-start | bytes 589832 | tf_op jit(solution)/shard_map/ppermute | solution.py:146
  39.5 3.3 %collective-permute-done.12 = bf16[192,512]{1,0:T(8,128)(2,1)S(1)} collective-permute-done((bf16[192,512]{1,0:T(8,128)(2,1)}, bf16[192,512]{1,0:T(8,128)(2,1)S(1)}, u32[]{:S(2)}, u32[]{:S(2)}) %collective-permute-start.12) | collective-permute-done | bytes 196640 | tf_op jit(solution)/shard_map/ppermute | solution.py:146
  43.0 10.6 %collective-permute-start.28 = (bf16[384,384]{1,0:T(8,128)(2,1)S(1)}, bf16[384,384]{1,0:T(8,128)(2,1)S(1)}, u32[]{:S(2)}, u32[]{:S(2)}) collective-permute-start(bf16[384,384]{1,0:T(8,128)(2,1)S(1)} %slice.53.own), channel_id=1, source_target_pairs={{0,16},{16,0},{32,48},{48,32},{1,17},{17,1},{33,49},{49,33},{2,18}... | collective-permute-start | bytes 884744 | tf_op jit(solution)/shard_map/ppermute | solution.py:40
  54.5 1.1 collective-permute-start.14
  56.5 2.7 %collective-permute-done.29.far = bf16[384,384]{1,0:T(8,128)(2,1)S(1)} collective-permute-done((bf16[384,384]{1,0:T(8,128)(2,1)S(1)}, bf16[384,384]{1,0:T(8,128)(2,1)S(1)}, u32[]{:S(2)}, u32[]{:S(2)}) %collective-permute-start.29) | collective-permute-done | bytes 294944 | tf_op jit(solution)/shard_map/ppermute | solution.py:40
  59.3 6.3 %collective-permute-start.22 = (bf16[384,512]{1,0:T(8,128)(2,1)S(1)}, bf16[384,512]{1,0:T(8,128)(2,1)S(1)}, u32[]{:S(2)}, u32[]{:S(2)}) collective-permute-start(bf16[384,512]{1,0:T(8,128)(2,1)S(1)} %slice.52.own), channel_id=1, source_target_pairs={{0,32},{16,48},{32,0},{48,16},{1,33},{17,49},{33,1},{49,17},{2,34}... | collective-permute-start | bytes 1179656 | tf_op jit(solution)/shard_map/ppermute | solution.py:40
  65.6 3.7 %collective-permute-start.21 = (bf16[384,512]{1,0:T(8,128)(2,1)S(1)}, bf16[384,512]{1,0:T(8,128)(2,1)S(1)}, u32[]{:S(2)}, u32[]{:S(2)}) collective-permute-start(bf16[384,512]{1,0:T(8,128)(2,1)S(1)} %slice.52.own), channel_id=1, source_target_pairs={{0,16},{16,0},{32,48},{48,32},{1,17},{17,1},{33,49},{49,33},{2,18}... | collective-permute-start | bytes 1179656 | tf_op jit(solution)/shard_map/ppermute | solution.py:40
  70.9 1.6 collective-permute-start.5
  73.5 16.1 %collective-permute-done.22.far = bf16[384,512]{1,0:T(8,128)(2,1)S(1)} collective-permute-done((bf16[384,512]{1,0:T(8,128)(2,1)S(1)}, bf16[384,512]{1,0:T(8,128)(2,1)S(1)}, u32[]{:S(2)}, u32[]{:S(2)}) %collective-permute-start.22) | collective-permute-done | bytes 393248 | tf_op jit(solution)/shard_map/ppermute | solution.py:40
  89.6 2.8 %collective-permute-start.16 = (bf16[192,512]{1,0:T(8,128)(2,1)S(1)}, bf16[192,512]{1,0:T(8,128)(2,1)S(1)}, u32[]{:S(2)}, u32[]{:S(2)}) collective-permute-start(bf16[192,512]{1,0:T(8,128)(2,1)S(1)} %slice_bitcast_fusion.1), channel_id=1, source_target_pairs={{0,6},{2,4},{4,2},{6,0},{1,7},{3,5},{5,3},{7,1},{8,14},{10,12},{12... | collective-permute-start | bytes 589832 | tf_op jit(solution)/shard_map/ppermute | solution.py:40
  93.9 1.3 collective-permute-start.24
  96.4 1.3 collective-permute-start.31
  98.6 1.8 %collective-permute-start.4 = (bf16[2,192,512]{2,1,0:T(8,128)(2,1)}, bf16[2,192,512]{2,1,0:T(8,128)(2,1)}, u32[]{:S(2)}, u32[]{:S(2)}) collective-permute-start(bf16[2,192,512]{2,1,0:T(8,128)(2,1)} %collective-permute-done.3.refs_2_), channel_id=1, source_target_pairs={{0,1},{1,0},{2,3},{3,2},{4,5},{5,4},{6,7},{7,6},{8,9},{9,8},{10,11... | collective-permute-start | bytes 1179656 | tf_op jit(solution)/shard_map/ppermute | solution.py:40
  100.4 11.9 %collective-permute-done.31.passed = bf16[384,384]{1,0:T(8,128)(2,1)S(1)} collective-permute-done((bf16[384,384]{1,0:T(8,128)(2,1)S(1)}, bf16[384,384]{1,0:T(8,128)(2,1)S(1)}, u32[]{:S(2)}, u32[]{:S(2)}) %collective-permute-start.31) | collective-permute-done | bytes 294944 | tf_op jit(solution)/shard_map/ppermute | solution.py:164
  113.0 1.3 collective-permute-start.8
  124.8 2.3 %grads.1 = (bf16[1536,512]{1,0:T(8,128)(2,1)S(1)}, bf16[1536,512]{1,0:T(8,128)(2,1)S(1)}, bf16[1536,512]{1,0:T(8,128)(2,1)S(1)}, bf16[1536,512]{1,0:T(8,128)(2,1)S(1)}) custom-call(s32[1]{0:T(128)} %bitcast.at_ref, bf16[2,192,512]{2,1,0:T(8,128)(2,1)S(1)} %pad_maximum_fusion.refs_0_, bf16[2,192,512]{2,1,0:T(8,128)(2,1)S(1)} %copy-done.12, ...), custom_call_target="tpu_custom_call" | custom-call | flops 2000000000 | bytes 12000000 | tf_op jit(solution)/shard_map/grads/pallas_call | solution.py:71
  131.2 3.0 %collective-permute-start.32 = (bf16[512,384]{1,0:T(8,128)(2,1)S(1)}, bf16[512,384]{1,0:T(8,128)(2,1)S(1)}, u32[]{:S(2)}, u32[]{:S(2)}) collective-permute-start(bf16[512,384]{1,0:T(8,128)(2,1)S(1)} %convolution_convert_fusion.5), channel_id=1, source_target_pairs={{0,128},{64,192},{128,0},{192,64},{1,129},{65,193},{129,1},{193,65... | collective-permute-start | bytes 1179656 | tf_op jit(solution)/shard_map/ppermute | solution.py:40
  135.6 1.7 collective-permute-start.25
  137.2 1.9 %collective-permute-start.27 = (bf16[512,512]{1,0:T(8,128)(2,1)S(1)}, bf16[512,512]{1,0:T(8,128)(2,1)S(1)}, u32[]{:S(2)}, u32[]{:S(2)}) collective-permute-start(bf16[512,512]{1,0:T(8,128)(2,1)S(1)} %convolution_convert_fusion), channel_id=1, source_target_pairs={{0,192},{64,128},{128,64},{192,0},{1,193},{65,129},{129,65},{193,1... | collective-permute-start | bytes 1572872 | tf_op jit(solution)/shard_map/ppermute | solution.py:40
  141.1 21.5 %collective-permute-done.25 = bf16[512,512]{1,0:T(8,128)(2,1)S(1)} collective-permute-done((bf16[512,512]{1,0:T(8,128)(2,1)S(1)}, bf16[512,512]{1,0:T(8,128)(2,1)S(1)}, u32[]{:S(2)}, u32[]{:S(2)}) %collective-permute-start.25) | collective-permute-done | bytes 524320 | tf_op jit(solution)/shard_map/ppermute | solution.py:40
  162.7 2.7 %collective-permute-start.34 = (bf16[512,384]{1,0:T(8,128)(2,1)S(1)}, bf16[512,384]{1,0:T(8,128)(2,1)S(1)}, u32[]{:S(2)}, u32[]{:S(2)}) collective-permute-start(bf16[512,384]{1,0:T(8,128)(2,1)S(1)} %convolution_convert_fusion.3), channel_id=1, source_target_pairs={{0,192},{64,128},{128,64},{192,0},{1,193},{65,129},{129,65},{193,1... | collective-permute-start | bytes 1179656 | tf_op jit(solution)/shard_map/ppermute | solution.py:40
  165.4 8.8 %collective-permute-done.26 = bf16[512,512]{1,0:T(8,128)(2,1)S(1)} collective-permute-done((bf16[512,512]{1,0:T(8,128)(2,1)S(1)}, bf16[512,512]{1,0:T(8,128)(2,1)S(1)}, u32[]{:S(2)}, u32[]{:S(2)}) %collective-permute-start.26) | collective-permute-done | bytes 524320 | tf_op jit(solution)/shard_map/ppermute | solution.py:40
  174.2 1.1 fusion.8.done
  175.4 1.2 add.88
  (125 shorter events, 30.7 us)
Async XLA Ops:
  3.2 16.6 %collective-permute-start.1 = (bf16[192,512]{1,0:T(8,128)(2,1)}, bf16[192,512]{1,0:T(8,128)(2,1)}, u32[]{:S(2)}, u32[]{:S(2)}) collective-permute-start(bf16[192,512]{1,0:T(8,128)(2,1)} %bitcast.4), channel_id=1, source_target_pairs={{0,8},{1,25},{2,42},{3,59},{4,12},{5,29},{6,46},{7,63},{8,0},{9,17... | collective-permute-start | bytes 589832 | tf_op jit(solution)/shard_map/ppermute | solution.py:146
  10.5 9.4 %collective-permute-start = (bf16[192,512]{1,0:T(8,128)(2,1)}, bf16[192,512]{1,0:T(8,128)(2,1)}, u32[]{:S(2)}, u32[]{:S(2)}) collective-permute-start(bf16[192,512]{1,0:T(8,128)(2,1)} %bitcast.4), channel_id=1, source_target_pairs={{0,0},{1,17},{2,34},{3,51},{4,4},{5,21},{6,38},{7,55},{8,8},{9,25}... | collective-permute-start | bytes 589832 | tf_op jit(solution)/shard_map/ppermute | solution.py:146
  14.1 14.7 %collective-permute-start.10 = (bf16[192,512]{1,0:T(8,128)(2,1)S(1)}, bf16[192,512]{1,0:T(8,128)(2,1)}, u32[]{:S(2)}, u32[]{:S(2)}) collective-permute-start(bf16[192,512]{1,0:T(8,128)(2,1)S(1)} %bitcast.63), channel_id=1, source_target_pairs={{0,2},{2,0},{4,6},{6,4},{1,3},{3,1},{5,7},{7,5},{8,10},{10,8},{12,... | collective-permute-start | bytes 589832 | tf_op jit(solution)/shard_map/ppermute | solution.py:40
  20.9 32.7 %collective-permute-start.6 = (bf16[2,192,512]{2,1,0:T(8,128)(2,1)S(1)}, bf16[2,192,512]{2,1,0:T(8,128)(2,1)S(1)}, u32[]{:S(2)}, u32[]{:S(2)}) collective-permute-start(bf16[2,192,512]{2,1,0:T(8,128)(2,1)S(1)} %pad_maximum_fusion.refs_0_), channel_id=1, source_target_pairs={{0,6},{2,4},{4,2},{6,0},{1,7},{3,5},{5,3},{7,1},{8,14},{10,12},{12... | collective-permute-start | bytes 1179656 | tf_op jit(solution)/shard_map/ppermute | solution.py:40
  28.2 26.3 %collective-permute-start.3 = (bf16[2,192,512]{2,1,0:T(8,128)(2,1)S(1)}, bf16[2,192,512]{2,1,0:T(8,128)(2,1)}, u32[]{:S(2)}, u32[]{:S(2)}) collective-permute-start(bf16[2,192,512]{2,1,0:T(8,128)(2,1)S(1)} %pad_maximum_fusion.refs_0_), channel_id=1, source_target_pairs={{0,2},{2,0},{4,6},{6,4},{1,3},{3,1},{5,7},{7,5},{8,10},{10,8},{12,... | collective-permute-start | bytes 1179656 | tf_op jit(solution)/shard_map/ppermute | solution.py:40
  28.8 14.1 %collective-permute-start.12 = (bf16[192,512]{1,0:T(8,128)(2,1)}, bf16[192,512]{1,0:T(8,128)(2,1)S(1)}, u32[]{:S(2)}, u32[]{:S(2)}) collective-permute-start(bf16[192,512]{1,0:T(8,128)(2,1)} %collective-permute-done.10), channel_id=1, source_target_pairs={{0,42},{1,59},{2,8},{3,25},{4,46},{5,63},{6,12},{7,29},{8,34},{9,5... | collective-permute-start | bytes 589832 | tf_op jit(solution)/shard_map/ppermute | solution.py:146
  30.4 12.7 %collective-permute-start.11 = (bf16[192,512]{1,0:T(8,128)(2,1)}, bf16[192,512]{1,0:T(8,128)(2,1)S(1)}, u32[]{:S(2)}, u32[]{:S(2)}) collective-permute-start(bf16[192,512]{1,0:T(8,128)(2,1)} %collective-permute-done.10), channel_id=1, source_target_pairs={{0,34},{1,51},{2,0},{3,17},{4,38},{5,55},{6,4},{7,21},{8,42},{9,59... | collective-permute-start | bytes 589832 | tf_op jit(solution)/shard_map/ppermute | solution.py:146
  38.8 15.0 %collective-permute-start.30 = (bf16[384,384]{1,0:T(8,128)(2,1)S(1)}, bf16[384,384]{1,0:T(8,128)(2,1)S(1)}, u32[]{:S(2)}, u32[]{:S(2)}) collective-permute-start(bf16[384,384]{1,0:T(8,128)(2,1)S(1)} %slice.53.own), channel_id=1, source_target_pairs={{16,32},{32,16},{17,33},{33,17},{18,34},{34,18},{19,35},{35,19},{2... | collective-permute-start | bytes 884744 | tf_op jit(solution)/shard_map/ppermute | solution.py:163
  42.8 16.4 %collective-permute-start.29 = (bf16[384,384]{1,0:T(8,128)(2,1)S(1)}, bf16[384,384]{1,0:T(8,128)(2,1)S(1)}, u32[]{:S(2)}, u32[]{:S(2)}) collective-permute-start(bf16[384,384]{1,0:T(8,128)(2,1)S(1)} %slice.53.own), channel_id=1, source_target_pairs={{0,32},{16,48},{32,0},{48,16},{1,33},{17,49},{33,1},{49,17},{2,34}... | collective-permute-start | bytes 884744 | tf_op jit(solution)/shard_map/ppermute | solution.py:40
  43.0 27.2 %collective-permute-start.28 = (bf16[384,384]{1,0:T(8,128)(2,1)S(1)}, bf16[384,384]{1,0:T(8,128)(2,1)S(1)}, u32[]{:S(2)}, u32[]{:S(2)}) collective-permute-start(bf16[384,384]{1,0:T(8,128)(2,1)S(1)} %slice.53.own), channel_id=1, source_target_pairs={{0,16},{16,0},{32,48},{48,32},{1,17},{17,1},{33,49},{49,33},{2,18}... | collective-permute-start | bytes 884744 | tf_op jit(solution)/shard_map/ppermute | solution.py:40
  53.7 11.9 %collective-permute-start.17 = (bf16[2,192,512]{2,1,0:T(8,128)(2,1)S(1)}, bf16[2,192,512]{2,1,0:T(8,128)(2,1)}, u32[]{:S(2)}, u32[]{:S(2)}) collective-permute-start(bf16[2,192,512]{2,1,0:T(8,128)(2,1)S(1)} %pad_maximum_fusion.2.refs_8_), channel_id=1, source_target_pairs={{0,6},{2,4},{4,2},{6,0},{1,7},{3,5},{5,3},{7,1},{8,14},{10,12},{12... | collective-permute-start | bytes 1179656 | tf_op jit(solution)/shard_map/ppermute | solution.py:40
  53.8 17.1 %collective-permute-start.23 = (bf16[384,512]{1,0:T(8,128)(2,1)S(1)}, bf16[384,512]{1,0:T(8,128)(2,1)S(1)}, u32[]{:S(2)}, u32[]{:S(2)}) collective-permute-start(bf16[384,512]{1,0:T(8,128)(2,1)S(1)} %slice.52.own), channel_id=1, source_target_pairs={{16,32},{32,16},{17,33},{33,17},{18,34},{34,18},{19,35},{35,19},{2... | collective-permute-start | bytes 1179656 | tf_op jit(solution)/shard_map/ppermute | solution.py:163
  54.5 18.0 %collective-permute-start.14 = (bf16[2,192,512]{2,1,0:T(8,128)(2,1)S(1)}, bf16[2,192,512]{2,1,0:T(8,128)(2,1)}, u32[]{:S(2)}, u32[]{:S(2)}) collective-permute-start(bf16[2,192,512]{2,1,0:T(8,128)(2,1)S(1)} %pad_maximum_fusion.2.refs_8_), channel_id=1, source_target_pairs={{0,2},{2,0},{4,6},{6,4},{1,3},{3,1},{5,7},{7,5},{8,10},{10,8},{12,... | collective-permute-start | bytes 1179656 | tf_op jit(solution)/shard_map/ppermute | solution.py:40
  59.3 30.3 %collective-permute-start.22 = (bf16[384,512]{1,0:T(8,128)(2,1)S(1)}, bf16[384,512]{1,0:T(8,128)(2,1)S(1)}, u32[]{:S(2)}, u32[]{:S(2)}) collective-permute-start(bf16[384,512]{1,0:T(8,128)(2,1)S(1)} %slice.52.own), channel_id=1, source_target_pairs={{0,32},{16,48},{32,0},{48,16},{1,33},{17,49},{33,1},{49,17},{2,34}... | collective-permute-start | bytes 1179656 | tf_op jit(solution)/shard_map/ppermute | solution.py:40
  65.6 26.8 %collective-permute-start.21 = (bf16[384,512]{1,0:T(8,128)(2,1)S(1)}, bf16[384,512]{1,0:T(8,128)(2,1)S(1)}, u32[]{:S(2)}, u32[]{:S(2)}) collective-permute-start(bf16[384,512]{1,0:T(8,128)(2,1)S(1)} %slice.52.own), channel_id=1, source_target_pairs={{0,16},{16,0},{32,48},{48,32},{1,17},{17,1},{33,49},{49,33},{2,18}... | collective-permute-start | bytes 1179656 | tf_op jit(solution)/shard_map/ppermute | solution.py:40
  70.9 23.0 %collective-permute-start.7 = (bf16[192,512]{1,0:T(8,128)(2,1)S(1)}, bf16[192,512]{1,0:T(8,128)(2,1)S(1)}, u32[]{:S(2)}, u32[]{:S(2)}) collective-permute-start(bf16[192,512]{1,0:T(8,128)(2,1)S(1)} %slice_bitcast_fusion.2), channel_id=1, source_target_pairs={{0,2},{2,0},{4,6},{6,4},{1,3},{3,1},{5,7},{7,5},{8,10},{10,8},{12,... | collective-permute-start | bytes 589832 | tf_op jit(solution)/shard_map/ppermute | solution.py:40
  70.9 23.0 %collective-permute-start.5 = (bf16[192,512]{1,0:T(8,128)(2,1)S(1)}, bf16[192,512]{1,0:T(8,128)(2,1)S(1)}, u32[]{:S(2)}, u32[]{:S(2)}) collective-permute-start(bf16[192,512]{1,0:T(8,128)(2,1)S(1)} %slice_bitcast_fusion.3), channel_id=1, source_target_pairs={{0,6},{2,4},{4,2},{6,0},{1,7},{3,5},{5,3},{7,1},{8,14},{10,12},{12... | collective-permute-start | bytes 589832 | tf_op jit(solution)/shard_map/ppermute | solution.py:40
  72.5 22.7 %collective-permute-start.18 = (bf16[192,512]{1,0:T(8,128)(2,1)S(1)}, bf16[192,512]{1,0:T(8,128)(2,1)S(1)}, u32[]{:S(2)}, u32[]{:S(2)}) collective-permute-start(bf16[192,512]{1,0:T(8,128)(2,1)S(1)} %slice_bitcast_fusion), channel_id=1, source_target_pairs={{0,2},{2,0},{4,6},{6,4},{1,3},{3,1},{5,7},{7,5},{8,10},{10,8},{12,... | collective-permute-start | bytes 589832 | tf_op jit(solution)/shard_map/ppermute | solution.py:40
  93.9 20.5 %collective-permute-start.13 = (bf16[2,192,512]{2,1,0:T(8,128)(2,1)S(1)}, bf16[2,192,512]{2,1,0:T(8,128)(2,1)S(1)}, u32[]{:S(2)}, u32[]{:S(2)}) collective-permute-start(bf16[2,192,512]{2,1,0:T(8,128)(2,1)S(1)} %pad_maximum_fusion.2.refs_8_), channel_id=1, source_target_pairs={{0,1},{1,0},{2,3},{3,2},{4,5},{5,4},{6,7},{7,6},{8,9},{9,8},{10,11... | collective-permute-start | bytes 1179656 | tf_op jit(solution)/shard_map/ppermute | solution.py:40
  93.9 21.2 %collective-permute-start.24 = (bf16[384,512]{1,0:T(8,128)(2,1)S(1)}, bf16[384,512]{1,0:T(8,128)(2,1)S(1)}, u32[]{:S(2)}, u32[]{:S(2)}) collective-permute-start(bf16[384,512]{1,0:T(8,128)(2,1)S(1)} %collective-permute-done.22.far), channel_id=1, source_target_pairs={{32,48},{16,0},{33,49},{17,1},{34,50},{18,2},{35,51},{19,3},{36,52... | collective-permute-start | bytes 1179656 | tf_op jit(solution)/shard_map/ppermute | solution.py:164
  95.2 21.2 %collective-permute-start.9 = (bf16[2,192,512]{2,1,0:T(8,128)(2,1)S(1)}, bf16[2,192,512]{2,1,0:T(8,128)(2,1)S(1)}, u32[]{:S(2)}, u32[]{:S(2)}) collective-permute-start(bf16[2,192,512]{2,1,0:T(8,128)(2,1)S(1)} %collective-permute-done.6.refs_6_), channel_id=1, source_target_pairs={{0,1},{1,0},{2,3},{3,2},{4,5},{5,4},{6,7},{7,6},{8,9},{9,8},{10,11... | collective-permute-start | bytes 1179656 | tf_op jit(solution)/shard_map/ppermute | solution.py:40
  96.4 15.9 %collective-permute-start.31 = (bf16[384,384]{1,0:T(8,128)(2,1)S(1)}, bf16[384,384]{1,0:T(8,128)(2,1)S(1)}, u32[]{:S(2)}, u32[]{:S(2)}) collective-permute-start(bf16[384,384]{1,0:T(8,128)(2,1)S(1)} %collective-permute-done.29.far), channel_id=1, source_target_pairs={{32,48},{16,0},{33,49},{17,1},{34,50},{18,2},{35,51},{19,3},{36,52... | collective-permute-start | bytes 884744 | tf_op jit(solution)/shard_map/ppermute | solution.py:164
  98.6 25.5 %collective-permute-start.4 = (bf16[2,192,512]{2,1,0:T(8,128)(2,1)}, bf16[2,192,512]{2,1,0:T(8,128)(2,1)}, u32[]{:S(2)}, u32[]{:S(2)}) collective-permute-start(bf16[2,192,512]{2,1,0:T(8,128)(2,1)} %collective-permute-done.3.refs_2_), channel_id=1, source_target_pairs={{0,1},{1,0},{2,3},{3,2},{4,5},{5,4},{6,7},{7,6},{8,9},{9,8},{10,11... | collective-permute-start | bytes 1179656 | tf_op jit(solution)/shard_map/ppermute | solution.py:40
  113.0 11.1 %collective-permute-start.8 = (bf16[2,192,512]{2,1,0:T(8,128)(2,1)S(1)}, bf16[2,192,512]{2,1,0:T(8,128)(2,1)}, u32[]{:S(2)}, u32[]{:S(2)}) collective-permute-start(bf16[2,192,512]{2,1,0:T(8,128)(2,1)S(1)} %pad_maximum_fusion.1.refs_4_), channel_id=1, source_target_pairs={{0,1},{1,0},{2,3},{3,2},{4,5},{5,4},{6,7},{7,6},{8,9},{9,8},{10,11... | collective-permute-start | bytes 1179656 | tf_op jit(solution)/shard_map/ppermute | solution.py:40
  115.1 9.0 %collective-permute-start.20 = (bf16[2,192,512]{2,1,0:T(8,128)(2,1)}, bf16[2,192,512]{2,1,0:T(8,128)(2,1)}, u32[]{:S(2)}, u32[]{:S(2)}) collective-permute-start(bf16[2,192,512]{2,1,0:T(8,128)(2,1)} %collective-permute-done.17.refs_14_), channel_id=1, source_target_pairs={{0,1},{1,0},{2,3},{3,2},{4,5},{5,4},{6,7},{7,6},{8,9},{9,8},{10,11... | collective-permute-start | bytes 1179656 | tf_op jit(solution)/shard_map/ppermute | solution.py:40
  115.9 8.2 %collective-permute-start.15 = (bf16[2,192,512]{2,1,0:T(8,128)(2,1)}, bf16[2,192,512]{2,1,0:T(8,128)(2,1)}, u32[]{:S(2)}, u32[]{:S(2)}) collective-permute-start(bf16[2,192,512]{2,1,0:T(8,128)(2,1)} %collective-permute-done.14.refs_10_), channel_id=1, source_target_pairs={{0,1},{1,0},{2,3},{3,2},{4,5},{5,4},{6,7},{7,6},{8,9},{9,8},{10,11... | collective-permute-start | bytes 1179656 | tf_op jit(solution)/shard_map/ppermute | solution.py:40
  131.2 44.2 %collective-permute-start.32 = (bf16[512,384]{1,0:T(8,128)(2,1)S(1)}, bf16[512,384]{1,0:T(8,128)(2,1)S(1)}, u32[]{:S(2)}, u32[]{:S(2)}) collective-permute-start(bf16[512,384]{1,0:T(8,128)(2,1)S(1)} %convolution_convert_fusion.5), channel_id=1, source_target_pairs={{0,128},{64,192},{128,0},{192,64},{1,129},{65,193},{129,1},{193,65... | collective-permute-start | bytes 1179656 | tf_op jit(solution)/shard_map/ppermute | solution.py:40
  134.2 41.2 %collective-permute-start.33 = (bf16[512,384]{1,0:T(8,128)(2,1)S(1)}, bf16[512,384]{1,0:T(8,128)(2,1)S(1)}, u32[]{:S(2)}, u32[]{:S(2)}) collective-permute-start(bf16[512,384]{1,0:T(8,128)(2,1)S(1)} %convolution_convert_fusion.4), channel_id=1, source_target_pairs={{0,64},{64,0},{128,192},{192,128},{1,65},{65,1},{129,193},{193,129... | collective-permute-start | bytes 1179656 | tf_op jit(solution)/shard_map/ppermute | solution.py:40
  135.6 27.1 %collective-permute-start.25 = (bf16[512,512]{1,0:T(8,128)(2,1)S(1)}, bf16[512,512]{1,0:T(8,128)(2,1)S(1)}, u32[]{:S(2)}, u32[]{:S(2)}) collective-permute-start(bf16[512,512]{1,0:T(8,128)(2,1)S(1)} %convolution_convert_fusion.2), channel_id=1, source_target_pairs={{0,128},{64,192},{128,0},{192,64},{1,129},{65,193},{129,1},{193,65... | collective-permute-start | bytes 1572872 | tf_op jit(solution)/shard_map/ppermute | solution.py:40
  137.2 37.0 %collective-permute-start.26 = (bf16[512,512]{1,0:T(8,128)(2,1)S(1)}, bf16[512,512]{1,0:T(8,128)(2,1)S(1)}, u32[]{:S(2)}, u32[]{:S(2)}) collective-permute-start(bf16[512,512]{1,0:T(8,128)(2,1)S(1)} %convolution_convert_fusion.1), channel_id=1, source_target_pairs={{0,64},{64,0},{128,192},{192,128},{1,65},{65,1},{129,193},{193,129... | collective-permute-start | bytes 1572872 | tf_op jit(solution)/shard_map/ppermute | solution.py:40
  137.2 37.0 %collective-permute-start.27 = (bf16[512,512]{1,0:T(8,128)(2,1)S(1)}, bf16[512,512]{1,0:T(8,128)(2,1)S(1)}, u32[]{:S(2)}, u32[]{:S(2)}) collective-permute-start(bf16[512,512]{1,0:T(8,128)(2,1)S(1)} %convolution_convert_fusion), channel_id=1, source_target_pairs={{0,192},{64,128},{128,64},{192,0},{1,193},{65,129},{129,65},{193,1... | collective-permute-start | bytes 1572872 | tf_op jit(solution)/shard_map/ppermute | solution.py:40
  162.7 12.7 %collective-permute-start.34 = (bf16[512,384]{1,0:T(8,128)(2,1)S(1)}, bf16[512,384]{1,0:T(8,128)(2,1)S(1)}, u32[]{:S(2)}, u32[]{:S(2)}) collective-permute-start(bf16[512,384]{1,0:T(8,128)(2,1)S(1)} %convolution_convert_fusion.3), channel_id=1, source_target_pairs={{0,192},{64,128},{128,64},{192,0},{1,193},{65,129},{129,65},{193,1... | collective-permute-start | bytes 1179656 | tf_op jit(solution)/shard_map/ppermute | solution.py:40
  (30 other events, 248.0 us)
